TPU v7x, 32 devices: a whole 2x2x4 slice. The times are simulated.
32 devices in a mesh: pool: 2 (over x), dp: 4 (over z), mp: 4 (over y, core).
Axes of the slice: x: 2, y: 2, z: 4, core: 2. Of those that a mesh axis runs over, the one named last changes fastest.
Arguments:
- states: bfloat16 [2, 4, 512, 8192], P('pool', 'dp', 'mp'), may hold values from -8 to 8
- lengths: int32 [2, 4], P(None, 'dp'), may hold values from 128 to 512
- gain: bfloat16 [2, 8192], replicated, may hold values from 0.099609375 to 1.8984375
- w_query: bfloat16 [2, 8192, 4096], P('pool', ('dp', 'mp')), may hold values from -0.088388348 to 0.088388348
- w_keyval: bfloat16 [2, 8192, 1024], P('pool', ('dp', 'mp')), may hold values from -0.088388348 to 0.088388348
Outputs:
- attended: bfloat16 [2, 4, 512, 4096], P('pool', 'dp', None, 'mp')
Inputs may be any that keep to these rules, and one draw needn't show every extreme that they name: `lengths`: live positions of each rollout; positions from it on are padding.
All inputs are finite; a program needn't handle non-finite values.
Results may differ from a plain program's by a relative error of at most 0.011.
Values may be sent and summed in bfloat16 or wider, within the bound.
No kernel may reach another device: no remote copies, remote signals or barrier semaphores. Data moves between devices by JAX's collectives and lax.ppermute only.
A program may use at most 128 MiB of HBM per device.

v0:
```python
import math

import jax
import jax.numpy as jnp
from jax import lax
from jax.sharding import PartitionSpec as P

HD = 128
QH = 32
KVH = 4


def partner(value, axis, distance):
    return lax.ppermute(value, axis, [(i, i ^ 1 << distance) for i in range(lax.axis_size(axis))])


def normalize(rows, gain_row):
    values = rows.astype(jnp.float32)
    meansq = jnp.mean(values * values, axis=-1, keepdims=True)
    return (values * lax.rsqrt(meansq + 1e-05) * gain_row.astype(jnp.float32)).astype(jnp.bfloat16)


def attend(query, keyval, length):
    seqlen = query.shape[0]
    local_heads = keyval.shape[1] // (2 * HD)
    groups = QH // KVH
    block = min(seqlen, 512)
    paired = keyval.reshape(seqlen, local_heads, 2 * HD)
    keys = paired[:, :, :HD]
    values = paired[:, :, HD:]
    places = jnp.arange(seqlen, dtype=jnp.int32)

    def one_block(index):
        start = index * block
        rows = query.reshape(block, local_heads, groups, HD)
        scores = jnp.einsum(
            "tkgd,skd->kgts", rows, keys, preferred_element_type=jnp.float32
        ) / math.sqrt(HD)
        qplaces = start + jnp.arange(block, dtype=jnp.int32)
        allowed = (places[None, :] <= qplaces[:, None]) & (places[None, :] < length)
        scores = jnp.where(allowed, scores, jnp.float32(-1e30))
        peak = jnp.max(scores, axis=-1, keepdims=True)
        expo = jnp.exp(scores - peak)
        probs = (expo / jnp.sum(expo, axis=-1, keepdims=True)).astype(jnp.bfloat16)
        result = jnp.einsum("kgts,skd->tkgd", probs, values, preferred_element_type=jnp.float32)
        result = result * (qplaces < length).astype(jnp.float32)[:, None, None, None]
        return result.reshape(block, local_heads * groups * HD).astype(jnp.bfloat16)

    blocks = lax.map(one_block, jnp.arange(seqlen // block, dtype=jnp.int32))
    return blocks.reshape(seqlen, local_heads * groups * HD)


def on_device(states, lengths, gain, w_query, w_keyval):
    own = lax.axis_index("pool")
    other = 1 - own
    normed = normalize(states, lax.dynamic_index_in_dim(gain, own, 0, keepdims=False))
    local_rows = lax.all_gather(normed, "mp", axis=2, tiled=True)
    whole = partner(local_rows, "pool", 0)
    rollouts = whole.shape[1]
    seqlen = whole.shape[2]
    tokens = whole[0].reshape(rollouts * seqlen, whole.shape[3])
    rows_query, rows_keyval = partner((w_query, w_keyval), "pool", 0)
    query_cols, keyval_cols = (
        lax.all_to_all(rows_query, "mp", split_axis=2, concat_axis=1, tiled=True),
        lax.all_to_all(rows_keyval, "mp", split_axis=2, concat_axis=1, tiled=True),
    )
    width_query = query_cols.shape[2]
    width_keyval = keyval_cols.shape[2]
    full_query, full_keyval = (
        lax.all_gather(query_cols, "dp", axis=1, tiled=True),
        lax.all_gather(keyval_cols, "dp", axis=1, tiled=True),
    )
    query = jnp.dot(tokens, full_query[0], preferred_element_type=jnp.float32)
    keyval = jnp.dot(tokens, full_keyval[0], preferred_element_type=jnp.float32)
    query = query.astype(jnp.bfloat16).reshape(rollouts, seqlen, width_query)
    keyval = keyval.astype(jnp.bfloat16).reshape(rollouts, seqlen, width_keyval)
    live = lax.dynamic_index_in_dim(lengths, other, 0, keepdims=False)
    attended = jax.vmap(attend)(query, keyval, live)
    return attended[None]


def solution(mesh):
    in_specs = (
        P("pool", "dp", "mp", None),
        P(None, "dp"),
        P(),
        P("pool", ("dp", "mp"), None),
        P("pool", ("dp", "mp"), None),
    )
    out_specs = P("pool", "dp", None, "mp")
    return jax.shard_map(
        on_device, mesh=mesh, in_specs=in_specs, out_specs=out_specs, check_vma=False
    )
```

profile of v0, /device:TPU:0, one launch (start us, length us, event | category | flops | bytes accessed | tf_op | source)
XLA Modules:
  0.0 573.3 jit_solution(5611344158581876059)
XLA Ops:
  6.5 0.0 copy-start
  6.5 0.0 all-gather.4.cloned.1.call-start
  6.5 2.2 fusion.7
  8.7 0.8 dynamic-slice_convert_fusion
  9.5 3.5 fusion.9
  13.1 0.0 all-gather.4.cloned.1.call-update
  13.1 0.0 all-gather.6.cloned.1.call-start
  13.1 0.0 copy-done.2
  13.2 3.0 collective-permute-start.1
  16.2 0.1 collective-permute-start.2
  16.3 23.9 %collective-permute-done.1 = bf16[1,512,1024]{2,1,0:T(8,128)(2,1)S(1)} collective-permute-done((bf16[1,512,1024]{2,1,0:T(8,128)(2,1)S(1)}, bf16[1,512,1024]{2,1,0:T(8,128)(2,1)S(1)}, u32[]{:S(2)}, u32[]{:S(2)}) %collective-permute-start.1) | collective-permute-done | bytes 1048608 | tf_op jit(solution)/shard_map/ppermute | solution.py:14
  40.2 1.8 copy.30
  42.0 0.6 broadcast.68
  42.6 7.3 %reduce.4 = bf16[1024,512]{1,0:T(8,128)(2,1)S(1)} reduce(bf16[1024,1,512]{2,1,0:T(2,128)(2,1)S(1)} %bitcast.94, bf16[]{:T(256)} %broadcast.68), dimensions={1}, to_apply=%bitcast.83.reduce_sub_computation | reduce | bytes 2097154
  49.9 0.8 reshape.124
  50.7 29.2 %all_to_all.36 = bf16[4,2,65536]{2,1,0:T(2,128)(2,1)S(1)} all-to-all(bf16[4,2,65536]{2,1,0:T(2,128)(2,1)S(1)} %reshape.124), channel_id=1, replica_groups=mesh['pool'=2,'dp'=4,'mp'=4] {'mp'}, dimensions={0} | all-to-all | bytes 2097152 | tf_op jit(solution)/shard_map/all_to_all | solution.py:65
  79.9 1.0 reshape.125
  80.9 0.3 copy.41
  81.2 1.3 copy.31
  82.5 0.0 all-gather.6.cloned.1.call-update
  82.5 0.2 all-gather.8.cloned.1.call-start
  82.7 46.6 %collective-permute-done.2 = bf16[1,512,4096]{2,1,0:T(8,128)(2,1)} collective-permute-done((bf16[1,512,4096]{2,1,0:T(8,128)(2,1)}, bf16[1,512,4096]{2,1,0:T(8,128)(2,1)}, u32[]{:S(2)}, u32[]{:S(2)}) %collective-permute-start.2) | collective-permute-done | bytes 4194336 | tf_op jit(solution)/shard_map/ppermute | solution.py:14
  129.3 18.9 %copy.32 = bf16[1,512,4096]{1,0,2:T(2,128)(2,1)} copy(bf16[1,512,4096]{2,1,0:T(8,128)(2,1)} %collective-permute-done.2) | data formatting | bytes 8388608 | tf_op jit(solution)/shard_map/ppermute | solution.py:14
  148.2 28.5 %reduce.3 = bf16[4096,512]{1,0:T(8,128)(2,1)} reduce(bf16[4096,1,512]{2,1,0:T(2,128)(2,1)} %bitcast.89, bf16[]{:T(256)} %broadcast.68), dimensions={1}, to_apply=%bitcast.81.reduce_sub_computation | reduce | bytes 8388610
  176.7 6.2 %reshape.122 = bf16[4,2,262144]{2,1,0:T(2,128)(2,1)} reshape(bf16[4096,512]{1,0:T(8,128)(2,1)} %reduce.3) | data formatting | bytes 8388608
  182.9 53.8 %all_to_all.37 = bf16[4,2,262144]{2,1,0:T(2,128)(2,1)} all-to-all(bf16[4,2,262144]{2,1,0:T(2,128)(2,1)} %reshape.122), channel_id=1, replica_groups=mesh['pool'=2,'dp'=4,'mp'=4] {'mp'}, dimensions={0} | all-to-all | bytes 8388608 | tf_op jit(solution)/shard_map/all_to_all | solution.py:64
  236.8 7.4 %reshape.123 = bf16[4096,1,512]{2,1,0:T(2,128)(2,1)} reshape(bf16[4,2,262144]{2,1,0:T(2,128)(2,1)} %all_to_all.37) | data formatting | bytes 8388608
  244.2 6.6 %copy.42 = bf16[1,512,4096]{1,2,0:T(8,128)(2,1)} copy(bf16[1,512,4096]{1,0,2:T(2,128)(2,1)} %bitcast.90) | data formatting | bytes 8388608
  250.8 6.3 %copy.33 = bf16[1,4,512,1024]{3,2,1,0:T(8,128)(2,1)} copy(bf16[1,4,512,1024]{2,3,1,0:T(8,128)(2,1)} %bitcast.91) | data formatting | bytes 8388608 | tf_op jit(solution)/shard_map/all_to_all | solution.py:64
  257.1 0.0 all-gather.8.cloned.1.call-update
  257.1 0.0 all-gather.4.cloned.1.call-done
  257.2 1.8 collective-permute-start
  259.0 0.0 copy-done
  259.0 0.6 constant_dynamic-slice_fusion
  259.6 0.6 iota_compare_fusion.1
  260.2 0.6 fusion.43
  260.9 0.1 fusion.40
  261.0 0.0 all-gather.6.cloned.1.call-done
  261.0 178.3 %collective-permute-done = bf16[1,1,512,8192]{3,2,1,0:T(8,128)(2,1)} collective-permute-done((bf16[1,1,512,8192]{3,2,1,0:T(8,128)(2,1)}, bf16[1,1,512,8192]{3,2,1,0:T(8,128)(2,1)}, u32[]{:S(2)}, u32[]{:S(2)}) %collective-permute-start) | collective-permute-done | bytes 8388640 | tf_op jit(solution)/shard_map/ppermute | solution.py:14
  439.4 6.9 %fusion.32 = bf16[1,512,1,256]{3,1,2,0:T(8,128)(2,1)S(1)} fusion(bf16[1,8192,256]{2,1,0:T(8,128)(2,1)} %all-gather.6.cloned.1.call-done, bf16[1,1,512,8192]{3,2,1,0:T(8,128)(2,1)} %collective-permute-done), kind=kOutput, calls=%fused_computation.24 | convolution fusion | flops 2147614720 | bytes 12845056 | tf_op jit(solution)/shard_map/dot_general | solution.py:74
  446.3 98.3 %all-gather.8.cloned.1.call-done = bf16[1,8192,1024]{2,1,0:T(8,128)(2,1)} async-done(((bf16[1,2048,1024]{2,1,0:T(8,128)(2,1)}), bf16[1,8192,1024]{2,1,0:T(8,128)(2,1)}) %all-gather.8.cloned.1.call-update) | async-done | bytes 16777232 | tf_op jit(solution)/shard_map/all_gather | solution.py:70
  544.6 14.8 %fusion.22 = bf16[64,8,8,128]{3,2,1,0:T(8,128)(2,1)S(1)} fusion(bf16[1,8192,1024]{2,1,0:T(8,128)(2,1)} %all-gather.8.cloned.1.call-done, bf16[1,1,512,8192]{3,2,1,0:T(8,128)(2,1)} %collective-permute-done), kind=kOutput, calls=%fused_computation.22 | convolution fusion | flops 8590458880 | bytes 26214400 | tf_op jit(solution)/shard_map/dot_general | solution.py:73
  559.4 1.6 fusion.6
  561.0 1.8 fusion.5
  562.8 0.0 copy-start.1
  562.8 2.7 fusion.14
  565.4 1.3 copy.37
  566.8 0.0 copy-done.1
  (2 shorter events, 0.0 us)
Async XLA Ops:
  6.5 252.4 %copy-start = (s32[2,1]{0,1:T(1,128)S(1)}, s32[2,1]{0,1:T(1,128)}, u32[]{:S(2)}) copy-start(s32[2,1]{0,1:T(1,128)} %param.6) | copy-start | bytes 28
  6.5 6.6 %copy-start.2 = (bf16[1,512,1024]{2,1,0:T(8,128)(2,1)S(1)}, bf16[1,512,1024]{2,1,0:T(8,128)(2,1)}, u32[]{:S(2)}) copy-start(bf16[1,512,1024]{2,1,0:T(8,128)(2,1)} %param.9) | copy-start | bytes 3145732
  6.5 250.6 %all-gather.4.cloned.1.call-start = ((), (), s32[]{:S(2)}) async-start(), calls=%async_computation.2 | async-start | bytes 10485760 | tf_op jit(solution)/shard_map/all_gather | solution.py:57
  13.1 247.9 %all-gather.6.cloned.1.call-start = ((), (), s32[]{:S(2)}) async-start(), calls=%async_computation.3 | async-start | bytes 5242880 | tf_op jit(solution)/shard_map/all_gather | solution.py:71
  13.2 27.0 %collective-permute-start.1 = (bf16[1,512,1024]{2,1,0:T(8,128)(2,1)S(1)}, bf16[1,512,1024]{2,1,0:T(8,128)(2,1)S(1)}, u32[]{:S(2)}, u32[]{:S(2)}) collective-permute-start(bf16[1,512,1024]{2,1,0:T(8,128)(2,1)S(1)} %copy-done.2), channel_id=1, source_target_pairs={{0,16},{16,0},{1,17},{17,1},{2,18},{18,2},{3,19},{19,3},{4,20},{20... | collective-permute-start | bytes 3145736 | tf_op jit(solution)/shard_map/ppermute | solution.py:14
  16.2 113.1 %collective-permute-start.2 = (bf16[1,512,4096]{2,1,0:T(8,128)(2,1)}, bf16[1,512,4096]{2,1,0:T(8,128)(2,1)}, u32[]{:S(2)}, u32[]{:S(2)}) collective-permute-start(bf16[1,512,4096]{2,1,0:T(8,128)(2,1)} %param.8), channel_id=1, source_target_pairs={{0,16},{16,0},{1,17},{17,1},{2,18},{18,2},{3,19},{19,3},{4,20},{20... | collective-permute-start | bytes 12582920 | tf_op jit(solution)/shard_map/ppermute | solution.py:14
  82.5 462.1 %all-gather.8.cloned.1.call-start = ((), (), s32[]{:S(2)}) async-start(), calls=%async_computation.4 | async-start | bytes 20971520 | tf_op jit(solution)/shard_map/all_gather | solution.py:70
  257.2 182.2 %collective-permute-start = (bf16[1,1,512,8192]{3,2,1,0:T(8,128)(2,1)}, bf16[1,1,512,8192]{3,2,1,0:T(8,128)(2,1)}, u32[]{:S(2)}, u32[]{:S(2)}) collective-permute-start(bf16[1,1,512,8192]{3,2,1,0:T(8,128)(2,1)} %all-gather.4.cloned.1.call-done), channel_id=1, source_target_pairs={{0,16},{16,0},{1,17},{17,1},{2,18},{18,2},{3,19},{19,3},{4,20},{20... | collective-permute-start | bytes 25165832 | tf_op jit(solution)/shard_map/ppermute | solution.py:14
  562.8 4.0 copy-start.1
Sparse Core Ops, SparseCore 0:
  13.2 72.2 all-gather.3
  87.0 80.7 all-gather.5
  257.3 287.2 all-gather.7
where the time goes:
time: 575 us; the launch traced here: 573 us
  waiting for transfers between devices  347 us (60%)
  blocking collectives  83 us (14%)
  local copies, waits for them, and re-layouts  53.2 us (9%)
  other arithmetic  45.4 us (8%)
  matrix products  26 us (5%)
  between operations  13.2 us (2%)
    ppermute x3, waiting for transfers between devices, partner(): lax.ppermute(value, axis, [(i, i ^ 1 << distance) for i in range(lax.axis...  249 us
    all_gather x1, waiting for transfers between devices, on_device(): lax.all_gather(query_cols, 'dp', axis=1, tiled=True)  98.3 us
    all_to_all x1, blocking collectives, on_device(): lax.all_to_all(rows_query, 'mp', split_axis=2, concat_axis=1, tiled=True)  53.8 us
    unnamed x2, other arithmetic  35.7 us
    all_to_all x1, blocking collectives, on_device(): lax.all_to_all(rows_keyval, 'mp', split_axis=2, concat_axis=1, tiled=True)  29.2 us
    unnamed x13, local copies, waits for them, and re-layouts  22.9 us
    ppermute x2, local copies, waits for them, and re-layouts, partner(): lax.ppermute(value, axis, [(i, i ^ 1 << distance) for i in range(lax.axis...  20.7 us
    dot_general x1, matrix products, on_device(): query = jnp.dot(tokens, full_query[0], preferred_element_type=jnp.float32)  14.8 us
  transfers between devices with their start and end apart: 6, of which 4 were waited for; matrix products, arithmetic and copies ran while one was open for 17% of the time, Pallas kernels for 0%

commit v1 on v0

v1 whole, which is shorter than its diff:
```python
import functools
import math

import jax
import jax.numpy as jnp
from jax import lax
from jax.experimental import pallas as pl
from jax.experimental.pallas import tpu as pltpu
from jax.sharding import PartitionSpec as P

HD = 128
F32 = jnp.float32
BF16 = jnp.bfloat16


def swap(value, axis, bits):
    return lax.ppermute(value, axis, [(i, i ^ bits) for i in range(lax.axis_size(axis))])


def normalize(rows, gain_row):
    values = rows.astype(F32)
    meansq = jnp.mean(values * values, axis=-1, keepdims=True)
    return (values * lax.rsqrt(meansq + 1e-05) * gain_row.astype(F32)).astype(BF16)


SMEM = pl.BlockSpec(memory_space=pltpu.SMEM)
NEAR = pl.BlockSpec(memory_space=pltpu.VMEM)
ANY = pl.BlockSpec(memory_space=pl.ANY)
ALONE = pltpu.CompilerParams(vmem_limit_bytes=62 << 20)


def whole(shape):
    return pl.BlockSpec(shape, lambda i: (0,) * len(shape))


def limit(held):
    return pltpu.CompilerParams(vmem_limit_bytes=held + (2 << 20))


def cost(flops, moved, exps=0):
    return pl.CostEstimate(flops=flops, bytes_accessed=moved, transcendentals=exps)


def columns_copies(target, span, kv_width, q_width, w_query, w_keyval, out, sems):
    copies, at = [], 0
    if span.start < kv_width:
        at = kv_width - span.start
        cols = pl.ds(pl.multiple_of(target * kv_width + span.start, HD), at)
        copies.append(pltpu.make_async_copy(w_keyval.at[:, cols], out.at[:, :at], sems.at[0]))
    lo, width = max(span.start, kv_width) - kv_width, span.stop - span.start
    cols = pl.ds(pl.multiple_of(target * q_width + lo, HD), width - at)
    copies.append(pltpu.make_async_copy(w_query.at[:, cols], out.at[:, at:], sems.at[1]))
    return copies


class Cuts:
    def __init__(self, wanted, widths, depth):
        self.wanted, self.widths = wanted, widths
        shapes = [(depth, span.stop - span.start) for _, span in wanted]
        self.out_shape = [jax.ShapeDtypeStruct(shape, BF16) for shape in shapes]
        self.scratch = [pltpu.VMEM(shape, BF16) for shape in shapes]
        self.scratch += [pltpu.SemaphoreType.DMA((len(wanted), 2)), pltpu.SemaphoreType.DMA((len(wanted),))]
        self.moved = sum(4 * rows * cols for rows, cols in shapes)

    def start(self, w_query, w_keyval, outs, scratch):
        me = lax.axis_index("mp")
        held, sems, out_sems = scratch[:-2], scratch[-2], scratch[-1]
        self.inward = [
            columns_copies(me ^ bits, span, *self.widths, w_query, w_keyval, held[i], sems.at[i])
            for i, (bits, span) in enumerate(self.wanted)
        ]
        self.outward = [pltpu.make_async_copy(held[i], outs[i], out_sems.at[i]) for i in range(len(outs))]
        for copies in self.inward:
            for copy in copies:
                copy.start()

    def pass_on(self):
        for copies, out in zip(self.inward, self.outward):
            for copy in copies:
                copy.wait()
            out.start()

    def finish(self):
        for out in self.outward:
            out.wait()


def cut_kernel(cuts, w_query, w_keyval, *refs):
    count = len(cuts.wanted)
    cuts.start(w_query, w_keyval, refs[:count], refs[count:])
    cuts.pass_on()
    cuts.finish()


def cut(cuts, w_query, w_keyval):
    return pl.pallas_call(
        functools.partial(cut_kernel, cuts),
        out_shape=cuts.out_shape,
        in_specs=[ANY, ANY],
        out_specs=[ANY] * len(cuts.wanted),
        scratch_shapes=cuts.scratch,
        compiler_params=ALONE,
        cost_estimate=cost(0, cuts.moved),
        name="cut",
    )(w_query, w_keyval)


def stack_kernel(spans, *refs):
    me = lax.axis_index("mp")
    blocks, o_ref, sems = refs[:-2], refs[-2], refs[-1]
    copies = []
    for r, (ref, span) in enumerate(zip(blocks, spans)):
        depth = ref.shape[0]
        rows = pl.ds(pl.multiple_of((me ^ r) * depth, depth), depth)
        copies.append(pltpu.make_async_copy(ref.at[:, span], o_ref.at[rows, :], sems.at[r]))
    for copy in copies:
        copy.start()
    for copy in copies:
        copy.wait()


def stack_rows(span, shared, blocks):
    depth = shared[0].shape[0]
    width = span.stop - span.start
    spans = [span] * len(shared) + [slice(0, width)] * len(blocks)
    shape = (depth * len(spans), width)
    return pl.pallas_call(
        functools.partial(stack_kernel, spans),
        out_shape=jax.ShapeDtypeStruct(shape, BF16),
        in_specs=[ANY] * len(spans),
        out_specs=NEAR,
        scratch_shapes=[pltpu.SemaphoreType.DMA((len(spans),))],
        compiler_params=limit(2 * shape[0] * width),
        cost_estimate=cost(0, 4 * shape[0] * width),
        name="stack",
    )(*shared, *blocks)


def begin_kernel(chunk, n, cuts, x_ref, gain_ref, w_query, w_keyval, *refs):
    count = len(cuts.wanted)
    outs, cut_outs, refs = refs[:n], refs[n : n + count], refs[n + count :]
    x_held, gain_held, scaled, sems, gain_sem, out_sems = refs[:6]
    own, z = lax.axis_index("pool"), lax.axis_index("dp")
    depth = outs[0].shape[1]
    pieces = [slice(at, at + chunk) for at in range(0, x_ref.shape[0], chunk)]
    copies = [pltpu.make_async_copy(x_ref.at[rows, :], x_held.at[rows, :], sems.at[i]) for i, rows in enumerate(pieces)]
    gain_copy = pltpu.make_async_copy(gain_ref, gain_held, gain_sem)
    copies[0].start()
    gain_copy.start()
    for copy in copies[1:]:
        copy.start()
    cuts.start(w_query, w_keyval, cut_outs, refs[6:])
    gain_copy.wait()
    gain_row = jnp.where(own == 0, gain_held[0:1, :].astype(F32), gain_held[1:2, :].astype(F32))
    outward = []
    for i, rows in enumerate(pieces):
        copies[i].wait()
        values = x_held[rows, :].astype(F32)
        meansq = jnp.mean(values * values, axis=-1, keepdims=True)
        scaled[rows, :] = (values * lax.rsqrt(meansq + 1e-05) * gain_row).astype(BF16)
        for s, o_ref in enumerate(outs):
            cols = pl.ds(pl.multiple_of((z ^ s) * depth, depth), depth)
            out = pltpu.make_async_copy(scaled.at[rows, cols], o_ref.at[rows, :], out_sems.at[i, s])
            out.start()
            outward.append(out)
        if i == len(pieces) // 2:
            cuts.pass_on()
    for out in outward:
        out.wait()
    cuts.finish()


def begin(rows, gain, w_query, w_keyval, n, cuts):
    count, width = rows.shape
    chunk = min(16, count)
    outs = pl.pallas_call(
        functools.partial(begin_kernel, chunk, n, cuts),
        out_shape=[jax.ShapeDtypeStruct((count, width // n), BF16)] * n + cuts.out_shape,
        in_specs=[ANY] * 4,
        out_specs=[ANY] * (n + len(cuts.wanted)),
        scratch_shapes=[
            pltpu.VMEM(rows.shape, BF16),
            pltpu.VMEM(gain.shape, BF16),
            pltpu.VMEM(rows.shape, BF16),
            pltpu.SemaphoreType.DMA((count // chunk,)),
            pltpu.SemaphoreType.DMA,
            pltpu.SemaphoreType.DMA((count // chunk, n)),
        ]
        + cuts.scratch,
        compiler_params=ALONE,
        cost_estimate=cost(4 * count * width, 4 * count * width + cuts.moved),
        name="begin",
    )(rows, gain, w_query, w_keyval)
    return outs[:n], outs[n:]


def project_kernel(sizes, added, *refs):
    count = sum(sizes)
    blocks, w_ref, more, refs = refs[:count], refs[count], refs[count + 1 :][: len(added)], refs[count + 1 + len(added) :]
    o_ref = refs[0]
    seqlen = o_ref.shape[0] // len(sizes)
    z = lax.axis_index("dp")
    middle = (z == 1) | (z == 2)
    for t, size in enumerate(sizes):
        mine, blocks = blocks[:size], blocks[size:]
        if size == 1:
            tokens = mine[0][...]
        else:
            rows = mine[0].shape[0]
            for i, ref in enumerate(mine):
                refs[1][i * rows : (i + 1) * rows, :] = ref[...]
            tokens = refs[1][...]
        total = jnp.dot(tokens, w_ref[...], preferred_element_type=F32)
        for ref, (start, masked) in zip(more, added):
            part = ref[start + t * seqlen : start + (t + 1) * seqlen, :].astype(F32)
            total = total + (jnp.where(middle, part, 0.0) if masked else part)
        o_ref[t * seqlen : (t + 1) * seqlen, :] = total.astype(BF16)


def project(tokens, weights, added=()):
    join = isinstance(tokens[0], list)
    groups = tokens if join else [[array] for array in tokens]
    depth, width = weights.shape
    seqlen = sum(block.shape[0] for block in groups[0])
    flat = [block for group in groups for block in group]
    rows = seqlen * len(groups)
    out_shape = [jax.ShapeDtypeStruct((rows, width), BF16)]
    if join:
        out_shape.append(jax.ShapeDtypeStruct((seqlen, depth), BF16))
    out = pl.pallas_call(
        functools.partial(
            project_kernel, [len(group) for group in groups], [(start, masked) for _, start, masked in added]
        ),
        out_shape=out_shape,
        in_specs=[NEAR] * (len(flat) + 1 + len(added)),
        out_specs=[NEAR] * len(out_shape),
        compiler_params=limit(4 << 20),
        cost_estimate=cost(2 * rows * depth * width, 2 * rows * depth + 2 * depth * width + 2 * rows * width),
        name="project",
    )(*flat, weights, *[array for array, _, _ in added])
    return out if join else out[0]


def attend_kernel(count, heads, skip, scalars, q_ref, kv_ref, o_ref, keys, values):
    me, length = scalars[0], scalars[1]
    seqlen = keys.shape[0]
    block = seqlen // count
    starts = [pl.multiple_of((b ^ me) * block, block) for b in range(count)]
    for b in range(count):
        keys[b * block : (b + 1) * block, :] = kv_ref[pl.ds(starts[b], block), :HD]
        values[b * block : (b + 1) * block, :] = kv_ref[pl.ds(starts[b], block), HD : 2 * HD]
    for b in range(count):
        reach = (b + 1) * block
        query = jnp.concatenate(
            [q_ref[pl.ds(starts[b], block), skip + h * HD : skip + (h + 1) * HD] for h in range(heads)], axis=0
        )
        scores = lax.dot_general(
            query, keys[:reach, :], (((1,), (1,)), ((), ())), preferred_element_type=F32
        ) * (1.0 / math.sqrt(HD))
        places = b * block + lax.rem(lax.broadcasted_iota(jnp.int32, (heads * block, 1), 0), block)
        last = jnp.minimum(places, length - 1)
        allowed = lax.broadcasted_iota(jnp.int32, (heads * block, reach), 1) <= last
        scores = jnp.where(allowed, scores, jnp.float32(-1e30))
        expo = jnp.exp(scores - jnp.max(scores, axis=-1, keepdims=True))
        probs = (expo * (1.0 / jnp.sum(expo, axis=-1, keepdims=True))).astype(BF16)
        result = jnp.dot(probs, values[:reach, :], preferred_element_type=F32)
        result = jnp.where(places < length, result, 0.0).astype(BF16)
        for h in range(heads):
            o_ref[b * block : reach, h * HD : (h + 1) * HD] = result[h * block : (h + 1) * block]


def attend(count, scalars, query, skip, heads, keyval):
    seqlen = keyval.shape[0]
    return pl.pallas_call(
        functools.partial(attend_kernel, count, heads, skip),
        out_shape=jax.ShapeDtypeStruct((seqlen, heads * HD), BF16),
        grid=(1,),
        in_specs=[SMEM, whole(query.shape), pl.BlockSpec((seqlen, 2 * HD), lambda i: (0, 0))],
        out_specs=whole((seqlen, heads * HD)),
        scratch_shapes=[pltpu.VMEM((seqlen, HD), BF16)] * 2,
        cost_estimate=cost(4 * seqlen * seqlen * HD * heads, 4 * seqlen * HD * heads, seqlen * seqlen * heads),
        compiler_params=limit(12 * seqlen * (query.shape[1] + seqlen * heads)),
        name="attend",
    )(scalars, query, keyval)


GROUP_HEADS = (2, 2, 2, 2)


def line_plan(states, lengths, gain, w_query, w_keyval):
    own = lax.axis_index("pool")
    n = lax.axis_size("dp")
    count = lax.axis_size("mp")
    me = lax.axis_index("mp")
    q_width = w_query.shape[2] // count
    kv_width = w_keyval.shape[2] // count
    w_query, w_keyval = w_query[0], w_keyval[0]

    spans, at = [], 0
    for g, heads in enumerate(GROUP_HEADS):
        to = at + heads * HD + (0 if g else kv_width)
        spans.append(slice(at, to))
        at = to

    widths = (kv_width, q_width)
    far = list(range(2, count))
    first = Cuts([(s, spans[0]) for s in far], widths, w_query.shape[0])
    normed, sent = begin(states[0, 0], gain, w_query, w_keyval, n, first)
    wanted = [(s, span) for span in spans[1:] for s in far] + [(bits, slice(0, at)) for bits in (0, 1)]
    *rest, mine, near = cut(Cuts(wanted, widths, w_query.shape[0]), w_query, w_keyval)
    sent = list(sent) + rest
    received = [[swap(sent[g * len(far) + i], "mp", s) for i, s in enumerate(far)] for g in range(len(spans))]
    near = swap(near, "mp", 1)
    weights = []
    for g, span in enumerate(spans):
        weights.append(stack_rows(span, [mine, near], received[g]))

    tokens = {}
    for s in range(n):
        piece = normed[s]
        if s:
            piece = swap(piece, "dp", s)
        blocks = {0: piece}
        bit = count // 2
        while bit:
            for have in list(blocks):
                blocks[have | bit] = swap(blocks[have], "mp", bit)
            bit //= 2
        tokens[s] = [blocks[j] for j in range(count)]

    def outer(value):
        return swap(value, "dp", 1)

    def inward(value, pairs=((0, 1), (3, 2))):
        return lax.ppermute(value, "dp", pairs)

    def inner(value):
        pairs = [(x * n + i, x * n + 3 - i) for x in range(2) for i in (1, 2)]
        pairs += [(x * n + i, (1 - x) * n + i) for x in range(2) for i in (0, 3)]
        return lax.ppermute(value, ("pool", "dp"), pairs)

    live = lax.dynamic_index_in_dim(lengths, own, 0, keepdims=False)
    scalars = jnp.stack([me.astype(jnp.int32), live[0]])
    seqlen = count * states.shape[2]
    pieces = []
    keyval = None
    for g, w in enumerate(weights):
        if g == 0:
            value, tokens[1] = project([tokens[1]], w)
            a1 = inward(value)
            value, tokens[3] = project([tokens[3]], w)
            c3 = inward(value)
            value, tokens[2] = project([tokens[2]], w)
            c2 = inward(value)
            b2 = inner(project([tokens[2]], w, [(c3, 0, False)]))
            b1 = inner(project([tokens[3]], w, [(c2, 0, False)]))
            d1 = inward(project([tokens[1]], w, [(b2, 0, False)]), ((1, 0), (2, 3)))
            total, tokens[0] = project([tokens[0]], w, [(a1, 0, False), (d1, 0, False), (b1, 0, True)])
            keyval = total
        else:
            s1 = inward(project([tokens[3], tokens[2]], w))
            s2 = inner(project([tokens[2], tokens[3]], w, [(s1, 0, False)]))
            s3 = outer(project([tokens[1]], w, [(s2, 0, True)]))
            total = project([tokens[0]], w, [(s3, 0, False), (s2, seqlen, True)])
        result = attend(count, scalars, total, 0 if g else kv_width, GROUP_HEADS[g], keyval)
        pieces.append(swap(result, "pool", 1))
    return jnp.concatenate(pieces, axis=1)[None, None]


def gather_plan(states, lengths, gain, w_query, w_keyval):
    own = lax.axis_index("pool")
    count = lax.axis_size("mp")
    normed = normalize(states, lax.dynamic_index_in_dim(gain, own, 0, keepdims=False))
    tokens = lax.all_gather(normed, "mp", axis=2, tiled=True)[0, 0]
    query, keyval = (
        jnp.dot(
            tokens,
            lax.all_gather(
                lax.all_to_all(w[0], "mp", split_axis=1, concat_axis=0, tiled=True), "dp", axis=0, tiled=True
            ),
            preferred_element_type=F32,
        ).astype(BF16)
        for w in (w_query, w_keyval)
    )
    live = lax.dynamic_index_in_dim(lengths, own, 0, keepdims=False)
    scalars = jnp.stack([jnp.int32(0), live[0]])
    result = attend(count, scalars, query, 0, query.shape[1] // HD, keyval)
    return swap(result, "pool", 1)[None, None]


def on_device(states, lengths, gain, w_query, w_keyval):
    n = lax.axis_size("dp")
    heads = w_query.shape[2] // lax.axis_size("mp") // HD
    if n == 4 and heads == sum(GROUP_HEADS):
        return line_plan(states, lengths, gain, w_query, w_keyval)
    return gather_plan(states, lengths, gain, w_query, w_keyval)


def solution(mesh):
    in_specs = (
        P("pool", "dp", "mp", None),
        P(None, "dp"),
        P(),
        P("pool", ("dp", "mp"), None),
        P("pool", ("dp", "mp"), None),
    )
    out_specs = P("pool", "dp", None, "mp")
    return jax.shard_map(
        on_device, mesh=mesh, in_specs=in_specs, out_specs=out_specs, check_vma=False
    )
```

time: 575 us -> 247 us (0.43)
  waiting for transfers between devices: 347 us -> 125 us
  blocking collectives: 83 us -> 0 us
  starting transfers between devices: 5.18 us -> 62.7 us
  Pallas kernels: 0 us -> 49.8 us
  local copies, waits for them, and re-layouts: 53.2 us -> 6.14 us
  other arithmetic: 45.4 us -> 1.88 us
  matrix products: 26 us -> 0 us
  between operations: 13.2 us -> 0.44 us
    ppermute x3 -> x43, waiting for transfers between devices: 249 us -> 125 us  [the longest x31 100 us: swap(): lax.ppermute(value, axis, [(i, i ^ bits) for i in range(lax.axis_size(axi...]
    all_gather x3 -> x0, waiting for transfers between devices: 98.3 us -> none  [the longest x1 98.3 us: on_device(): lax.all_gather(query_cols, 'dp', axis=1, tiled=True)]
    all_to_all x2 -> x0, blocking collectives: 83 us -> none  [the longest x1 53.8 us: on_device(): lax.all_to_all(rows_query, 'mp', split_axis=2, concat_axis=1, tiled=True)]
    ppermute x3 -> x43, starting transfers between devices: 4.91 us -> 62.7 us  [the longest x31 33.4 us: swap(): lax.ppermute(value, axis, [(i, i ^ bits) for i in range(lax.axis_size(axi...]
    pallas_call x0 -> x29, Pallas kernels: none -> 49.8 us  [the longest x19 27.6 us: project(): pl.pallas_call(functools.partial(project_kernel, [len(group) for group in...]
    unnamed x2 -> x0, other arithmetic: 35.7 us -> none
    dot_general x4 -> x0, matrix products: 26 us -> none  [the longest x1 14.8 us: on_device(): query = jnp.dot(tokens, full_query[0], preferred_element_type=jnp.float32)]
    ppermute x2 -> x0, local copies, waits for them, and re-layouts: 20.7 us -> none  [partner(): lax.ppermute(value, axis, [(i, i ^ 1 << distance) for i in range(lax.axis...]
  transfers between devices with their start and end apart: 6 -> 43, of which waited for: 4 -> 21; matrix products, arithmetic and copies ran while one was open for 17% -> 1% of each run, Pallas kernels for 0% -> 17%
where the time goes in v1:
time: 247 us; the launch traced here: 246 us
  waiting for transfers between devices  125 us (51%)
  starting transfers between devices  62.7 us (25%)
  Pallas kernels  49.8 us (20%)
  local copies, waits for them, and re-layouts  6.14 us (2%)
    ppermute x31, waiting for transfers between devices, swap(): lax.ppermute(value, axis, [(i, i ^ bits) for i in range(lax.axis_size(axi...  100 us
    ppermute x31, starting transfers between devices, swap(): lax.ppermute(value, axis, [(i, i ^ bits) for i in range(lax.axis_size(axi...  33.4 us
    pallas_call x19, Pallas kernels, project(): pl.pallas_call(functools.partial(project_kernel, [len(group) for group in...  27.6 us
    ppermute x7, waiting for transfers between devices, inward(): return lax.ppermute(value, 'dp', pairs)  25.3 us
    ppermute x7, starting transfers between devices, inward(): return lax.ppermute(value, 'dp', pairs)  21.8 us
    pallas_call x4, Pallas kernels, attend(): pl.pallas_call(functools.partial(attend_kernel, count, heads, skip), out_...  9.14 us
    ppermute x5, starting transfers between devices, inner(): return lax.ppermute(value, ('pool', 'dp'), pairs)  7.52 us
    unnamed x42, local copies, waits for them, and re-layouts  5.47 us
  transfers between devices with their start and end apart: 43, of which 21 were waited for; matrix products, arithmetic and copies ran while one was open for 1% of the time, Pallas kernels for 17%

profile of v1, /device:TPU:0, one launch (start us, length us, event | category | flops | bytes accessed | tf_op | source)
XLA Modules:
  0.0 246.3 jit_solution(8875341939823367966)
XLA Ops:
  0.0 4.2 %cut.1 = (bf16[512,256]{1,0:T(8,128)(2,1)}, bf16[512,256]{1,0:T(8,128)(2,1)}, bf16[512,256]{1,0:T(8,128)(2,1)}, bf16[512,256]{1,0:T(8,128)(2,1)}, bf16[512,256]{...) custom-call(bf16[512,4096]{1,0:T(8,128)(2,1)} %bitcast.7, ...), custom_call_target="tpu_custom_call" | custom-call | bytes 8388608 | tf_op jit(solution)/shard_map/cut/pallas_call | solution.py:96
  4.7 2.6 %collective-permute-start.25 = (bf16[512,256]{1,0:T(8,128)(2,1)}, bf16[512,256]{1,0:T(8,128)(2,1)S(1)}, u32[]{:S(2)}, u32[]{:S(2)}) collective-permute-start(bf16[512,256]{1,0:T(8,128)(2,1)} %get-tuple-element.43), channel_id=1, source_target_pairs={{0,2},{1,3},{2,0},{3,1},{4,6},{5,7},{6,4},{7,5},{8,10},{9,11},{10,... | collective-permute-start | bytes 786440 | tf_op jit(solution)/shard_map/ppermute | solution.py:17
  7.3 4.6 %begin.1 = (bf16[128,2048]{1,0:T(8,128)(2,1)}, bf16[128,2048]{1,0:T(8,128)(2,1)}, bf16[128,2048]{1,0:T(8,128)(2,1)}, bf16[128,2048]{1,0:T(8,128)(2,1)}, bf16[512...) custom-call(bf16[128,8192]{1,0:T(8,128)(2,1)} %bitcast.11, bf16[2,8192]{1,0:T(2,128)(2,1)} %gain_ref.1, ...), custom_call_target="tpu_custom_call" | custom-call | flops 4194304 | bytes 6291456 | tf_op jit(solution)/shard_map/begin/pallas_call | solution.py:176
  12.0 3.7 %collective-permute-start.15 = (bf16[128,2048]{1,0:T(8,128)(2,1)}, bf16[128,2048]{1,0:T(8,128)(2,1)S(1)}, u32[]{:S(2)}, u32[]{:S(2)}) collective-permute-start(bf16[128,2048]{1,0:T(8,128)(2,1)} %get-tuple-element.37), channel_id=1, source_target_pairs={{0,12},{4,8},{8,4},{12,0},{1,13},{5,9},{9,5},{13,1},{2,14},{6,10},... | collective-permute-start | bytes 1572872 | tf_op jit(solution)/shard_map/ppermute | solution.py:17
  15.7 1.5 collective-permute-start.31
  17.2 7.3 %collective-permute-done.26.refs_3_ = bf16[512,256]{1,0:T(8,128)(2,1)S(1)} collective-permute-done((bf16[512,256]{1,0:T(8,128)(2,1)}, bf16[512,256]{1,0:T(8,128)(2,1)S(1)}, u32[]{:S(2)}, u32[]{:S(2)}) %collective-permute-start.26) | collective-permute-done | bytes 262176 | tf_op jit(solution)/shard_map/ppermute | solution.py:17
  24.8 5.4 %collective-permute-done.31.refs_2_ = bf16[512,256]{1,0:T(8,128)(2,1)S(1)} collective-permute-done((bf16[512,256]{1,0:T(8,128)(2,1)}, bf16[512,256]{1,0:T(8,128)(2,1)S(1)}, u32[]{:S(2)}, u32[]{:S(2)}) %collective-permute-start.31) | collective-permute-done | bytes 262176 | tf_op jit(solution)/shard_map/ppermute | solution.py:17
  30.7 1.5 collective-permute-start.17
  32.2 3.5 %collective-permute-done.32.refs_3_ = bf16[512,256]{1,0:T(8,128)(2,1)S(1)} collective-permute-done((bf16[512,256]{1,0:T(8,128)(2,1)S(1)}, bf16[512,256]{1,0:T(8,128)(2,1)S(1)}, u32[]{:S(2)}, u32[]{:S(2)}) %collective-permute-start.32) | collective-permute-done | bytes 262176 | tf_op jit(solution)/shard_map/ppermute | solution.py:17
  35.9 25.1 %collective-permute-done.11.refs_0_ = bf16[128,2048]{1,0:T(8,128)(2,1)S(1)} collective-permute-done((bf16[128,2048]{1,0:T(8,128)(2,1)}, bf16[128,2048]{1,0:T(8,128)(2,1)S(1)}, u32[]{:S(2)}, u32[]{:S(2)}) %collective-permute-start.11) | collective-permute-done | bytes 524320 | tf_op jit(solution)/shard_map/ppermute | solution.py:17
  62.0 7.4 %collective-permute-done.5.refs_3_ = bf16[512,512]{1,0:T(8,128)(2,1)S(1)} collective-permute-done((bf16[512,512]{1,0:T(8,128)(2,1)}, bf16[512,512]{1,0:T(8,128)(2,1)S(1)}, u32[]{:S(2)}, u32[]{:S(2)}) %collective-permute-start.5) | collective-permute-done | bytes 524320 | tf_op jit(solution)/shard_map/ppermute | solution.py:17
  69.4 5.9 %collective-permute-start.6 = (bf16[128,2048]{1,0:T(8,128)(2,1)}, bf16[128,2048]{1,0:T(8,128)(2,1)S(1)}, u32[]{:S(2)}, u32[]{:S(2)}) collective-permute-start(bf16[128,2048]{1,0:T(8,128)(2,1)} %get-tuple-element.32), channel_id=1, source_target_pairs={{0,4},{4,0},{8,12},{12,8},{1,5},{5,1},{9,13},{13,9},{2,6},{6,2},{1... | collective-permute-start | bytes 1572872 | tf_op jit(solution)/shard_map/ppermute | solution.py:17
  75.3 5.4 %collective-permute-done.13.refs_2_ = bf16[128,2048]{1,0:T(8,128)(2,1)S(1)} collective-permute-done((bf16[128,2048]{1,0:T(8,128)(2,1)S(1)}, bf16[128,2048]{1,0:T(8,128)(2,1)S(1)}, u32[]{:S(2)}, u32[]{:S(2)}) %collective-permute-start.13) | collective-permute-done | bytes 524320 | tf_op jit(solution)/shard_map/ppermute | solution.py:17
  83.0 1.6 collective-permute-start.37
  87.3 2.5 %collective-permute-start.8 = (bf16[128,2048]{1,0:T(8,128)(2,1)S(1)}, bf16[128,2048]{1,0:T(8,128)(2,1)S(1)}, u32[]{:S(2)}, u32[]{:S(2)}) collective-permute-start(bf16[128,2048]{1,0:T(8,128)(2,1)S(1)} %collective-permute-done.6.refs_0_), channel_id=1, source_target_pairs={{0,2},{1,3},{2,0},{3,1},{4,6},{5,7},{6,4},{7,5},{8,10},{9,11},{10,... | collective-permute-start | bytes 1572872 | tf_op jit(solution)/shard_map/ppermute | solution.py:17
  89.8 3.8 %collective-permute-start.19 = (bf16[512,512]{1,0:T(8,128)(2,1)S(1)}, bf16[512,512]{1,0:T(8,128)(2,1)S(1)}, u32[]{:S(2)}, u32[]{:S(2)}) collective-permute-start(bf16[512,512]{1,0:T(8,128)(2,1)S(1)} %get-tuple-element.38), channel_id=1, source_target_pairs={{0,4},{12,8},{1,5},{13,9},{2,6},{14,10},{3,7},{15,11},{16,20},{28,... | collective-permute-start | bytes 1572872 | tf_op jit(solution)/shard_map/ppermute | solution.py:335
  96.0 6.9 %collective-permute-done.37.refs_2_ = bf16[512,256]{1,0:T(8,128)(2,1)S(1)} collective-permute-done((bf16[512,256]{1,0:T(8,128)(2,1)S(1)}, bf16[512,256]{1,0:T(8,128)(2,1)S(1)}, u32[]{:S(2)}, u32[]{:S(2)}) %collective-permute-start.37) | collective-permute-done | bytes 262176 | tf_op jit(solution)/shard_map/ppermute | solution.py:17
  104.1 13.8 %collective-permute-done.38.refs_3_ = bf16[512,256]{1,0:T(8,128)(2,1)S(1)} collective-permute-done((bf16[512,256]{1,0:T(8,128)(2,1)S(1)}, bf16[512,256]{1,0:T(8,128)(2,1)S(1)}, u32[]{:S(2)}, u32[]{:S(2)}) %collective-permute-start.38) | collective-permute-done | bytes 262176 | tf_op jit(solution)/shard_map/ppermute | solution.py:17
  117.9 7.1 %collective-permute-start.27 = (bf16[1024,256]{1,0:T(8,128)(2,1)S(1)}, bf16[1024,256]{1,0:T(8,128)(2,1)S(1)}, u32[]{:S(2)}, u32[]{:S(2)}) collective-permute-start(bf16[1024,256]{1,0:T(8,128)(2,1)S(1)} %project.26), channel_id=1, source_target_pairs={{0,4},{12,8},{1,5},{13,9},{2,6},{14,10},{3,7},{15,11},{16,20},{28,... | collective-permute-start | bytes 1572872 | tf_op jit(solution)/shard_map/ppermute | solution.py:335
  131.5 1.5 collective-permute-start.39
  134.3 1.5 collective-permute-start.22
  140.0 8.5 %collective-permute-done.33.refs_3_ = bf16[1024,256]{1,0:T(8,128)(2,1)S(1)} collective-permute-done((bf16[1024,256]{1,0:T(8,128)(2,1)S(1)}, bf16[1024,256]{1,0:T(8,128)(2,1)S(1)}, u32[]{:S(2)}, u32[]{:S(2)}) %collective-permute-start.33) | collective-permute-done | bytes 524320 | tf_op jit(solution)/shard_map/ppermute | solution.py:335
  149.8 1.6 collective-permute-start.28
  151.3 8.4 %collective-permute-done.39.refs_3_ = bf16[1024,256]{1,0:T(8,128)(2,1)S(1)} collective-permute-done((bf16[1024,256]{1,0:T(8,128)(2,1)S(1)}, bf16[1024,256]{1,0:T(8,128)(2,1)S(1)}, u32[]{:S(2)}, u32[]{:S(2)}) %collective-permute-start.39) | collective-permute-done | bytes 524320 | tf_op jit(solution)/shard_map/ppermute | solution.py:335
  159.7 1.5 collective-permute-start.34
  161.2 2.1 project.19
  163.4 2.0 project.35
  165.4 5.4 %collective-permute-done.22.refs_2_ = bf16[512,512]{1,0:T(8,128)(2,1)S(1)} collective-permute-done((bf16[512,512]{1,0:T(8,128)(2,1)S(1)}, bf16[512,512]{1,0:T(8,128)(2,1)S(1)}, u32[]{:S(2)}, u32[]{:S(2)}) %collective-permute-start.22) | collective-permute-done | bytes 524320 | tf_op jit(solution)/shard_map/ppermute | solution.py:335
  170.8 1.5 collective-permute-start.40
  172.3 2.0 project.24
  174.3 2.1 project.23
  177.2 5.3 %collective-permute-start.10 = (bf16[512,512]{1,0:T(8,128)(2,1)}, bf16[512,512]{1,0:T(8,128)(2,1)}, u32[]{:S(2)}, u32[]{:S(2)}) collective-permute-start(bf16[512,512]{1,0:T(8,128)(2,1)} %get-tuple-element.33), channel_id=1, source_target_pairs={{0,4},{12,8},{1,5},{13,9},{2,6},{14,10},{3,7},{15,11},{16,20},{28,... | collective-permute-start | bytes 1572872 | tf_op jit(solution)/shard_map/ppermute | solution.py:335
  186.7 1.6 copy-done.4
  192.1 3.5 %collective-permute-start.29 = (bf16[512,256]{1,0:T(8,128)(2,1)S(1)}, bf16[512,256]{1,0:T(8,128)(2,1)S(1)}, u32[]{:S(2)}, u32[]{:S(2)}) collective-permute-start(bf16[512,256]{1,0:T(8,128)(2,1)S(1)} %project.28), channel_id=1, source_target_pairs={{0,4},{4,0},{8,12},{12,8},{1,5},{5,1},{9,13},{13,9},{2,6},{6,2},{1... | collective-permute-start | bytes 786440 | tf_op jit(solution)/shard_map/ppermute | solution.py:17
  196.4 1.8 project.36
  198.2 2.0 collective-permute-start.41
  200.2 1.5 collective-permute-done.21.refs_6_
  201.8 3.0 %project.25 = (bf16[512,512]{1,0:T(8,128)(2,1)S(1)}, bf16[512,2048]{1,0:T(8,128)(2,1)S(1)}) custom-call(bf16[128,2048]{1,0:T(8,128)(2,1)S(1)} %copy-done.15, bf16[128,2048]{1,0:T(8,128)(2,1)S(1)} %copy-done.17, bf16[128,2048]{1,0:T(8,128)(2,1)} %collective-permute-done.1.refs_2_, bf16[128,2048]{1,0:T(8,128)(2,1)} %collective-permute-done.2.refs_3_, ...), custom_call_target="tpu_custom_call" | custom-call | flops 1073741824 | bytes 4718592 | tf_op jit(solution)/shard_map/project/pallas_call | solution.py:230
  204.8 2.3 attend.4
  208.0 2.3 attend.5
  210.3 2.6 %collective-permute-done.35.refs_2_ = bf16[512,256]{1,0:T(8,128)(2,1)S(1)} collective-permute-done((bf16[512,256]{1,0:T(8,128)(2,1)S(1)}, bf16[512,256]{1,0:T(8,128)(2,1)S(1)}, u32[]{:S(2)}, u32[]{:S(2)}) %collective-permute-start.35) | collective-permute-done | bytes 262176 | tf_op jit(solution)/shard_map/ppermute | solution.py:17
  213.6 2.3 attend.6
  217.2 1.8 project.37.q_ref
  219.0 2.3 attend.7
  225.4 5.1 %collective-permute-done.24 = bf16[512,256]{1,0:T(8,128)(2,1)S(1)} collective-permute-done((bf16[512,256]{1,0:T(8,128)(2,1)S(1)}, bf16[512,256]{1,0:T(8,128)(2,1)S(1)}, u32[]{:S(2)}, u32[]{:S(2)}) %collective-permute-start.24) | collective-permute-done | bytes 262176 | tf_op jit(solution)/shard_map/ppermute | solution.py:17
  230.5 5.6 %collective-permute-done.42 = bf16[512,256]{1,0:T(8,128)(2,1)S(1)} collective-permute-done((bf16[512,256]{1,0:T(8,128)(2,1)S(1)}, bf16[512,256]{1,0:T(8,128)(2,1)S(1)}, u32[]{:S(2)}, u32[]{:S(2)}) %collective-permute-start.42) | collective-permute-done | bytes 262176 | tf_op jit(solution)/shard_map/ppermute | solution.py:17
  236.1 5.6 %collective-permute-done.36 = bf16[512,256]{1,0:T(8,128)(2,1)S(1)} collective-permute-done((bf16[512,256]{1,0:T(8,128)(2,1)S(1)}, bf16[512,256]{1,0:T(8,128)(2,1)S(1)}, u32[]{:S(2)}, u32[]{:S(2)}) %collective-permute-start.36) | collective-permute-done | bytes 262176 | tf_op jit(solution)/shard_map/ppermute | solution.py:17
  241.7 3.5 %collective-permute-done.30 = bf16[512,256]{1,0:T(8,128)(2,1)S(1)} collective-permute-done((bf16[512,256]{1,0:T(8,128)(2,1)S(1)}, bf16[512,256]{1,0:T(8,128)(2,1)S(1)}, u32[]{:S(2)}, u32[]{:S(2)}) %collective-permute-start.30) | collective-permute-done | bytes 262176 | tf_op jit(solution)/shard_map/ppermute | solution.py:17
  (112 shorter events, 42.1 us)
Async XLA Ops:
  0.0 186.0 %copy-start = (s32[2,1]{0,1:T(1,128)S(1)}, s32[2,1]{0,1:T(1,128)}, u32[]{:S(2)}) copy-start(s32[2,1]{0,1:T(1,128)} %param.6) | copy-start | bytes 28
  4.2 76.5 %collective-permute-start.3 = (bf16[512,1280]{1,0:T(8,128)(2,1)}, bf16[512,1280]{1,0:T(8,128)(2,1)}, u32[]{:S(2)}, u32[]{:S(2)}) collective-permute-start(bf16[512,1280]{1,0:T(8,128)(2,1)} %get-tuple-element.29), channel_id=1, source_target_pairs={{0,1},{1,0},{2,3},{3,2},{4,5},{5,4},{6,7},{7,6},{8,9},{9,8},{10,11... | collective-permute-start | bytes 3932168 | tf_op jit(solution)/shard_map/ppermute | solution.py:17
  4.7 10.9 %collective-permute-start.25 = (bf16[512,256]{1,0:T(8,128)(2,1)}, bf16[512,256]{1,0:T(8,128)(2,1)S(1)}, u32[]{:S(2)}, u32[]{:S(2)}) collective-permute-start(bf16[512,256]{1,0:T(8,128)(2,1)} %get-tuple-element.43), channel_id=1, source_target_pairs={{0,2},{1,3},{2,0},{3,1},{4,6},{5,7},{6,4},{7,5},{8,10},{9,11},{10,... | collective-permute-start | bytes 786440 | tf_op jit(solution)/shard_map/ppermute | solution.py:17
  7.3 73.8 %copy-start.9 = (bf16[512,1280]{1,0:T(8,128)(2,1)S(1)}, bf16[512,1280]{1,0:T(8,128)(2,1)}, u32[]{:S(2)}) copy-start(bf16[512,1280]{1,0:T(8,128)(2,1)} %get-tuple-element.28.refs_0_) | copy-start | bytes 3932164
  12.0 18.7 %collective-permute-start.15 = (bf16[128,2048]{1,0:T(8,128)(2,1)}, bf16[128,2048]{1,0:T(8,128)(2,1)S(1)}, u32[]{:S(2)}, u32[]{:S(2)}) collective-permute-start(bf16[128,2048]{1,0:T(8,128)(2,1)} %get-tuple-element.37), channel_id=1, source_target_pairs={{0,12},{4,8},{8,4},{12,0},{1,13},{5,9},{9,5},{13,1},{2,14},{6,10},... | collective-permute-start | bytes 1572872 | tf_op jit(solution)/shard_map/ppermute | solution.py:17
  15.7 8.8 %collective-permute-start.26 = (bf16[512,256]{1,0:T(8,128)(2,1)}, bf16[512,256]{1,0:T(8,128)(2,1)S(1)}, u32[]{:S(2)}, u32[]{:S(2)}) collective-permute-start(bf16[512,256]{1,0:T(8,128)(2,1)} %get-tuple-element.44), channel_id=1, source_target_pairs={{0,3},{1,2},{2,1},{3,0},{4,7},{5,6},{6,5},{7,4},{8,11},{9,10},{10,... | collective-permute-start | bytes 786440 | tf_op jit(solution)/shard_map/ppermute | solution.py:17
  15.7 45.3 %collective-permute-start.11 = (bf16[128,2048]{1,0:T(8,128)(2,1)}, bf16[128,2048]{1,0:T(8,128)(2,1)S(1)}, u32[]{:S(2)}, u32[]{:S(2)}) collective-permute-start(bf16[128,2048]{1,0:T(8,128)(2,1)} %get-tuple-element.35), channel_id=1, source_target_pairs={{0,8},{4,12},{8,0},{12,4},{1,9},{5,13},{9,1},{13,5},{2,10},{6,14},... | collective-permute-start | bytes 1572872 | tf_op jit(solution)/shard_map/ppermute | solution.py:17
  15.7 14.5 %collective-permute-start.31 = (bf16[512,256]{1,0:T(8,128)(2,1)}, bf16[512,256]{1,0:T(8,128)(2,1)S(1)}, u32[]{:S(2)}, u32[]{:S(2)}) collective-permute-start(bf16[512,256]{1,0:T(8,128)(2,1)} %get-tuple-element.45), channel_id=1, source_target_pairs={{0,2},{1,3},{2,0},{3,1},{4,6},{5,7},{6,4},{7,5},{8,10},{9,11},{10,... | collective-permute-start | bytes 786440 | tf_op jit(solution)/shard_map/ppermute | solution.py:17
  24.4 11.2 %collective-permute-start.32 = (bf16[512,256]{1,0:T(8,128)(2,1)S(1)}, bf16[512,256]{1,0:T(8,128)(2,1)S(1)}, u32[]{:S(2)}, u32[]{:S(2)}) collective-permute-start(bf16[512,256]{1,0:T(8,128)(2,1)S(1)} %copy-done.20), channel_id=1, source_target_pairs={{0,3},{1,2},{2,1},{3,0},{4,7},{5,6},{6,5},{7,4},{8,11},{9,10},{10,... | collective-permute-start | bytes 786440 | tf_op jit(solution)/shard_map/ppermute | solution.py:17
  30.1 31.3 %collective-permute-start.4 = (bf16[512,512]{1,0:T(8,128)(2,1)}, bf16[512,512]{1,0:T(8,128)(2,1)S(1)}, u32[]{:S(2)}, u32[]{:S(2)}) collective-permute-start(bf16[512,512]{1,0:T(8,128)(2,1)} %get-tuple-element.30), channel_id=1, source_target_pairs={{0,2},{1,3},{2,0},{3,1},{4,6},{5,7},{6,4},{7,5},{8,10},{9,11},{10,... | collective-permute-start | bytes 1572872 | tf_op jit(solution)/shard_map/ppermute | solution.py:17
  30.7 30.8 %collective-permute-start.17 = (bf16[128,2048]{1,0:T(8,128)(2,1)S(1)}, bf16[128,2048]{1,0:T(8,128)(2,1)S(1)}, u32[]{:S(2)}, u32[]{:S(2)}) collective-permute-start(bf16[128,2048]{1,0:T(8,128)(2,1)S(1)} %collective-permute-done.15.refs_0_), channel_id=1, source_target_pairs={{0,2},{1,3},{2,0},{3,1},{4,6},{5,7},{6,4},{7,5},{8,10},{9,11},{10,... | collective-permute-start | bytes 1572872 | tf_op jit(solution)/shard_map/ppermute | solution.py:17
  35.7 33.7 %collective-permute-start.5 = (bf16[512,512]{1,0:T(8,128)(2,1)}, bf16[512,512]{1,0:T(8,128)(2,1)S(1)}, u32[]{:S(2)}, u32[]{:S(2)}) collective-permute-start(bf16[512,512]{1,0:T(8,128)(2,1)} %get-tuple-element.31), channel_id=1, source_target_pairs={{0,3},{1,2},{2,1},{3,0},{4,7},{5,6},{6,5},{7,4},{8,11},{9,10},{10,... | collective-permute-start | bytes 1572872 | tf_op jit(solution)/shard_map/ppermute | solution.py:17
  61.0 19.7 %collective-permute-start.13 = (bf16[128,2048]{1,0:T(8,128)(2,1)S(1)}, bf16[128,2048]{1,0:T(8,128)(2,1)S(1)}, u32[]{:S(2)}, u32[]{:S(2)}) collective-permute-start(bf16[128,2048]{1,0:T(8,128)(2,1)S(1)} %collective-permute-done.11.refs_0_), channel_id=1, source_target_pairs={{0,2},{1,3},{2,0},{3,1},{4,6},{5,7},{6,4},{7,5},{8,10},{9,11},{10,... | collective-permute-start | bytes 1572872 | tf_op jit(solution)/shard_map/ppermute | solution.py:17
  61.5 20.9 %collective-permute-start.16 = (bf16[128,2048]{1,0:T(8,128)(2,1)S(1)}, bf16[128,2048]{1,0:T(8,128)(2,1)S(1)}, u32[]{:S(2)}, u32[]{:S(2)}) collective-permute-start(bf16[128,2048]{1,0:T(8,128)(2,1)S(1)} %collective-permute-done.15.refs_0_), channel_id=1, source_target_pairs={{0,1},{1,0},{2,3},{3,2},{4,5},{5,4},{6,7},{7,6},{8,9},{9,8},{10,11... | collective-permute-start | bytes 1572872 | tf_op jit(solution)/shard_map/ppermute | solution.py:17
  61.5 21.5 %collective-permute-start.18 = (bf16[128,2048]{1,0:T(8,128)(2,1)S(1)}, bf16[128,2048]{1,0:T(8,128)(2,1)S(1)}, u32[]{:S(2)}, u32[]{:S(2)}) collective-permute-start(bf16[128,2048]{1,0:T(8,128)(2,1)S(1)} %collective-permute-done.17.refs_2_), channel_id=1, source_target_pairs={{0,1},{1,0},{2,3},{3,2},{4,5},{5,4},{6,7},{7,6},{8,9},{9,8},{10,11... | collective-permute-start | bytes 1572872 | tf_op jit(solution)/shard_map/ppermute | solution.py:17
  69.4 17.9 %collective-permute-start.6 = (bf16[128,2048]{1,0:T(8,128)(2,1)}, bf16[128,2048]{1,0:T(8,128)(2,1)S(1)}, u32[]{:S(2)}, u32[]{:S(2)}) collective-permute-start(bf16[128,2048]{1,0:T(8,128)(2,1)} %get-tuple-element.32), channel_id=1, source_target_pairs={{0,4},{4,0},{8,12},{12,8},{1,5},{5,1},{9,13},{13,9},{2,6},{6,2},{1... | collective-permute-start | bytes 1572872 | tf_op jit(solution)/shard_map/ppermute | solution.py:17
  80.6 9.1 %collective-permute-start.12 = (bf16[128,2048]{1,0:T(8,128)(2,1)S(1)}, bf16[128,2048]{1,0:T(8,128)(2,1)S(1)}, u32[]{:S(2)}, u32[]{:S(2)}) collective-permute-start(bf16[128,2048]{1,0:T(8,128)(2,1)S(1)} %collective-permute-done.11.refs_0_), channel_id=1, source_target_pairs={{0,1},{1,0},{2,3},{3,2},{4,5},{5,4},{6,7},{7,6},{8,9},{9,8},{10,11... | collective-permute-start | bytes 1572872 | tf_op jit(solution)/shard_map/ppermute | solution.py:17
  80.7 12.9 %collective-permute-start.14 = (bf16[128,2048]{1,0:T(8,128)(2,1)S(1)}, bf16[128,2048]{1,0:T(8,128)(2,1)S(1)}, u32[]{:S(2)}, u32[]{:S(2)}) collective-permute-start(bf16[128,2048]{1,0:T(8,128)(2,1)S(1)} %collective-permute-done.13.refs_2_), channel_id=1, source_target_pairs={{0,1},{1,0},{2,3},{3,2},{4,5},{5,4},{6,7},{7,6},{8,9},{9,8},{10,11... | collective-permute-start | bytes 1572872 | tf_op jit(solution)/shard_map/ppermute | solution.py:17
  82.4 92.0 %copy-start.1 = (bf16[2048,512]{1,0:T(8,128)(2,1)}, bf16[2048,512]{1,0:T(8,128)(2,1)S(1)}, u32[]{:S(2)}) copy-start(bf16[2048,512]{1,0:T(8,128)(2,1)S(1)} %stack.12.refs_4_.refs_1_) | copy-start | bytes 6291460
  82.4 45.9 %collective-permute-start.1 = (bf16[128,2048]{1,0:T(8,128)(2,1)S(1)}, bf16[128,2048]{1,0:T(8,128)(2,1)}, u32[]{:S(2)}, u32[]{:S(2)}) collective-permute-start(bf16[128,2048]{1,0:T(8,128)(2,1)S(1)} %copy-done.14), channel_id=1, source_target_pairs={{0,2},{1,3},{2,0},{3,1},{4,6},{5,7},{6,4},{7,5},{8,10},{9,11},{10,... | collective-permute-start | bytes 1572872 | tf_op jit(solution)/shard_map/ppermute | solution.py:17
  83.0 19.9 %collective-permute-start.37 = (bf16[512,256]{1,0:T(8,128)(2,1)S(1)}, bf16[512,256]{1,0:T(8,128)(2,1)S(1)}, u32[]{:S(2)}, u32[]{:S(2)}) collective-permute-start(bf16[512,256]{1,0:T(8,128)(2,1)S(1)} %copy-done.19), channel_id=1, source_target_pairs={{0,2},{1,3},{2,0},{3,1},{4,6},{5,7},{6,4},{7,5},{8,10},{9,11},{10,... | collective-permute-start | bytes 786440 | tf_op jit(solution)/shard_map/ppermute | solution.py:17
  87.3 43.7 %collective-permute-start.8 = (bf16[128,2048]{1,0:T(8,128)(2,1)S(1)}, bf16[128,2048]{1,0:T(8,128)(2,1)S(1)}, u32[]{:S(2)}, u32[]{:S(2)}) collective-permute-start(bf16[128,2048]{1,0:T(8,128)(2,1)S(1)} %collective-permute-done.6.refs_0_), channel_id=1, source_target_pairs={{0,2},{1,3},{2,0},{3,1},{4,6},{5,7},{6,4},{7,5},{8,10},{9,11},{10,... | collective-permute-start | bytes 1572872 | tf_op jit(solution)/shard_map/ppermute | solution.py:17
  89.8 41.7 %collective-permute-start.19 = (bf16[512,512]{1,0:T(8,128)(2,1)S(1)}, bf16[512,512]{1,0:T(8,128)(2,1)S(1)}, u32[]{:S(2)}, u32[]{:S(2)}) collective-permute-start(bf16[512,512]{1,0:T(8,128)(2,1)S(1)} %get-tuple-element.38), channel_id=1, source_target_pairs={{0,4},{12,8},{1,5},{13,9},{2,6},{14,10},{3,7},{15,11},{16,20},{28,... | collective-permute-start | bytes 1572872 | tf_op jit(solution)/shard_map/ppermute | solution.py:335
  93.6 24.3 %collective-permute-start.38 = (bf16[512,256]{1,0:T(8,128)(2,1)S(1)}, bf16[512,256]{1,0:T(8,128)(2,1)S(1)}, u32[]{:S(2)}, u32[]{:S(2)}) collective-permute-start(bf16[512,256]{1,0:T(8,128)(2,1)S(1)} %copy-done.18), channel_id=1, source_target_pairs={{0,3},{1,2},{2,1},{3,0},{4,7},{5,6},{6,5},{7,4},{8,11},{9,10},{10,... | collective-permute-start | bytes 786440 | tf_op jit(solution)/shard_map/ppermute | solution.py:17
  102.9 31.4 %collective-permute-start.7 = (bf16[128,2048]{1,0:T(8,128)(2,1)S(1)}, bf16[128,2048]{1,0:T(8,128)(2,1)S(1)}, u32[]{:S(2)}, u32[]{:S(2)}) collective-permute-start(bf16[128,2048]{1,0:T(8,128)(2,1)S(1)} %collective-permute-done.6.refs_0_), channel_id=1, source_target_pairs={{0,1},{1,0},{2,3},{3,2},{4,5},{5,4},{6,7},{7,6},{8,9},{9,8},{10,11... | collective-permute-start | bytes 1572872 | tf_op jit(solution)/shard_map/ppermute | solution.py:17
  102.9 22.1 %copy-start.10 = (bf16[512,1280]{1,0:T(8,128)(2,1)S(1)}, bf16[512,1280]{1,0:T(8,128)(2,1)}, u32[]{:S(2)}) copy-start(bf16[512,1280]{1,0:T(8,128)(2,1)} %get-tuple-element.28.refs_0_) | copy-start | bytes 3932164
  117.9 19.4 %collective-permute-start.27 = (bf16[1024,256]{1,0:T(8,128)(2,1)S(1)}, bf16[1024,256]{1,0:T(8,128)(2,1)S(1)}, u32[]{:S(2)}, u32[]{:S(2)}) collective-permute-start(bf16[1024,256]{1,0:T(8,128)(2,1)S(1)} %project.26), channel_id=1, source_target_pairs={{0,4},{12,8},{1,5},{13,9},{2,6},{14,10},{3,7},{15,11},{16,20},{28,... | collective-permute-start | bytes 1572872 | tf_op jit(solution)/shard_map/ppermute | solution.py:335
  127.1 21.4 %copy-start.6 = (bf16[2048,256]{1,0:T(8,128)(2,1)}, bf16[2048,256]{1,0:T(8,128)(2,1)S(1)}, u32[]{:S(2)}) copy-start(bf16[2048,256]{1,0:T(8,128)(2,1)S(1)} %stack.14.refs_2_.refs_1_) | copy-start | bytes 3145732
  128.3 20.2 %collective-permute-start.33 = (bf16[1024,256]{1,0:T(8,128)(2,1)S(1)}, bf16[1024,256]{1,0:T(8,128)(2,1)S(1)}, u32[]{:S(2)}, u32[]{:S(2)}) collective-permute-start(bf16[1024,256]{1,0:T(8,128)(2,1)S(1)} %project.30), channel_id=1, source_target_pairs={{0,4},{12,8},{1,5},{13,9},{2,6},{14,10},{3,7},{15,11},{16,20},{28,... | collective-permute-start | bytes 1572872 | tf_op jit(solution)/shard_map/ppermute | solution.py:335
  130.9 18.8 %collective-permute-start.9 = (bf16[128,2048]{1,0:T(8,128)(2,1)S(1)}, bf16[128,2048]{1,0:T(8,128)(2,1)S(1)}, u32[]{:S(2)}, u32[]{:S(2)}) collective-permute-start(bf16[128,2048]{1,0:T(8,128)(2,1)S(1)} %collective-permute-done.8.refs_2_), channel_id=1, source_target_pairs={{0,1},{1,0},{2,3},{3,2},{4,5},{5,4},{6,7},{7,6},{8,9},{9,8},{10,11... | collective-permute-start | bytes 1572872 | tf_op jit(solution)/shard_map/ppermute | solution.py:17
  131.5 28.3 %collective-permute-start.39 = (bf16[1024,256]{1,0:T(8,128)(2,1)S(1)}, bf16[1024,256]{1,0:T(8,128)(2,1)S(1)}, u32[]{:S(2)}, u32[]{:S(2)}) collective-permute-start(bf16[1024,256]{1,0:T(8,128)(2,1)S(1)} %project.34), channel_id=1, source_target_pairs={{0,4},{12,8},{1,5},{13,9},{2,6},{14,10},{3,7},{15,11},{16,20},{28,... | collective-permute-start | bytes 1572872 | tf_op jit(solution)/shard_map/ppermute | solution.py:335
  134.3 36.5 %collective-permute-start.22 = (bf16[512,512]{1,0:T(8,128)(2,1)S(1)}, bf16[512,512]{1,0:T(8,128)(2,1)S(1)}, u32[]{:S(2)}, u32[]{:S(2)}) collective-permute-start(bf16[512,512]{1,0:T(8,128)(2,1)S(1)} %get-tuple-element.40), channel_id=1, source_target_pairs={{0,4},{12,8},{1,5},{13,9},{2,6},{14,10},{3,7},{15,11},{16,20},{28,... | collective-permute-start | bytes 1572872 | tf_op jit(solution)/shard_map/ppermute | solution.py:335
  137.3 33.5 %collective-permute-start.20 = (bf16[512,512]{1,0:T(8,128)(2,1)S(1)}, bf16[512,512]{1,0:T(8,128)(2,1)S(1)}, u32[]{:S(2)}, u32[]{:S(2)}) collective-permute-start(bf16[512,512]{1,0:T(8,128)(2,1)S(1)} %project.22), channel_id=1, source_target_pairs={{4,8},{8,4},{20,24},{24,20},{0,16},{12,28},{16,0},{28,12},{5,9},{9... | collective-permute-start | bytes 1572872 | tf_op jit(solution)/shard_map/ppermute | solution.py:340
  148.5 27.9 %collective-permute-start = (bf16[128,2048]{1,0:T(8,128)(2,1)S(1)}, bf16[128,2048]{1,0:T(8,128)(2,1)S(1)}, u32[]{:S(2)}, u32[]{:S(2)}) collective-permute-start(bf16[128,2048]{1,0:T(8,128)(2,1)S(1)} %copy-done.14), channel_id=1, source_target_pairs={{0,1},{1,0},{2,3},{3,2},{4,5},{5,4},{6,7},{7,6},{8,9},{9,8},{10,11... | collective-permute-start | bytes 1572872 | tf_op jit(solution)/shard_map/ppermute | solution.py:17
  149.8 32.7 %collective-permute-start.28 = (bf16[1024,256]{1,0:T(8,128)(2,1)S(1)}, bf16[1024,256]{1,0:T(8,128)(2,1)S(1)}, u32[]{:S(2)}, u32[]{:S(2)}) collective-permute-start(bf16[1024,256]{1,0:T(8,128)(2,1)S(1)} %project.27), channel_id=1, source_target_pairs={{4,8},{8,4},{20,24},{24,20},{0,16},{12,28},{16,0},{28,12},{5,9},{9... | collective-permute-start | bytes 1572872 | tf_op jit(solution)/shard_map/ppermute | solution.py:340
  159.7 25.0 %collective-permute-start.34 = (bf16[1024,256]{1,0:T(8,128)(2,1)S(1)}, bf16[1024,256]{1,0:T(8,128)(2,1)S(1)}, u32[]{:S(2)}, u32[]{:S(2)}) collective-permute-start(bf16[1024,256]{1,0:T(8,128)(2,1)S(1)} %project.31), channel_id=1, source_target_pairs={{4,8},{8,4},{20,24},{24,20},{0,16},{12,28},{16,0},{28,12},{5,9},{9... | collective-permute-start | bytes 1572872 | tf_op jit(solution)/shard_map/ppermute | solution.py:340
  170.8 21.3 %collective-permute-start.2 = (bf16[128,2048]{1,0:T(8,128)(2,1)}, bf16[128,2048]{1,0:T(8,128)(2,1)}, u32[]{:S(2)}, u32[]{:S(2)}) collective-permute-start(bf16[128,2048]{1,0:T(8,128)(2,1)} %collective-permute-done.1.refs_2_), channel_id=1, source_target_pairs={{0,1},{1,0},{2,3},{3,2},{4,5},{5,4},{6,7},{7,6},{8,9},{9,8},{10,11... | collective-permute-start | bytes 1572872 | tf_op jit(solution)/shard_map/ppermute | solution.py:17
  170.8 24.8 %collective-permute-start.40 = (bf16[1024,256]{1,0:T(8,128)(2,1)}, bf16[1024,256]{1,0:T(8,128)(2,1)}, u32[]{:S(2)}, u32[]{:S(2)}) collective-permute-start(bf16[1024,256]{1,0:T(8,128)(2,1)} %project.35), channel_id=1, source_target_pairs={{4,8},{8,4},{20,24},{24,20},{0,16},{12,28},{16,0},{28,12},{5,9},{9... | collective-permute-start | bytes 1572872 | tf_op jit(solution)/shard_map/ppermute | solution.py:340
  177.2 21.0 %collective-permute-start.10 = (bf16[512,512]{1,0:T(8,128)(2,1)}, bf16[512,512]{1,0:T(8,128)(2,1)}, u32[]{:S(2)}, u32[]{:S(2)}) collective-permute-start(bf16[512,512]{1,0:T(8,128)(2,1)} %get-tuple-element.33), channel_id=1, source_target_pairs={{0,4},{12,8},{1,5},{13,9},{2,6},{14,10},{3,7},{15,11},{16,20},{28,... | collective-permute-start | bytes 1572872 | tf_op jit(solution)/shard_map/ppermute | solution.py:335
  183.3 17.0 %collective-permute-start.23 = (bf16[512,512]{1,0:T(8,128)(2,1)}, bf16[512,512]{1,0:T(8,128)(2,1)}, u32[]{:S(2)}, u32[]{:S(2)}) collective-permute-start(bf16[512,512]{1,0:T(8,128)(2,1)} %project.24), channel_id=1, source_target_pairs={{4,8},{8,4},{20,24},{24,20},{0,16},{12,28},{16,0},{28,12},{5,9},{9... | collective-permute-start | bytes 1572872 | tf_op jit(solution)/shard_map/ppermute | solution.py:340
  184.7 17.0 %collective-permute-start.21 = (bf16[512,512]{1,0:T(8,128)(2,1)}, bf16[512,512]{1,0:T(8,128)(2,1)}, u32[]{:S(2)}, u32[]{:S(2)}) collective-permute-start(bf16[512,512]{1,0:T(8,128)(2,1)} %project.23), channel_id=1, source_target_pairs={{4,0},{8,12},{5,1},{9,13},{6,2},{10,14},{7,3},{11,15},{20,16},{24,... | collective-permute-start | bytes 1572872 | tf_op jit(solution)/shard_map/ppermute | solution.py:335
  192.1 15.2 %collective-permute-start.29 = (bf16[512,256]{1,0:T(8,128)(2,1)S(1)}, bf16[512,256]{1,0:T(8,128)(2,1)S(1)}, u32[]{:S(2)}, u32[]{:S(2)}) collective-permute-start(bf16[512,256]{1,0:T(8,128)(2,1)S(1)} %project.28), channel_id=1, source_target_pairs={{0,4},{4,0},{8,12},{12,8},{1,5},{5,1},{9,13},{13,9},{2,6},{6,2},{1... | collective-permute-start | bytes 786440 | tf_op jit(solution)/shard_map/ppermute | solution.py:17
  195.6 17.3 %collective-permute-start.35 = (bf16[512,256]{1,0:T(8,128)(2,1)S(1)}, bf16[512,256]{1,0:T(8,128)(2,1)S(1)}, u32[]{:S(2)}, u32[]{:S(2)}) collective-permute-start(bf16[512,256]{1,0:T(8,128)(2,1)S(1)} %project.32), channel_id=1, source_target_pairs={{0,4},{4,0},{8,12},{12,8},{1,5},{5,1},{9,13},{13,9},{2,6},{6,2},{1... | collective-permute-start | bytes 786440 | tf_op jit(solution)/shard_map/ppermute | solution.py:17
  198.2 19.0 %collective-permute-start.41 = (bf16[512,256]{1,0:T(8,128)(2,1)S(1)}, bf16[512,256]{1,0:T(8,128)(2,1)S(1)}, u32[]{:S(2)}, u32[]{:S(2)}) collective-permute-start(bf16[512,256]{1,0:T(8,128)(2,1)S(1)} %project.36), channel_id=1, source_target_pairs={{0,4},{4,0},{8,12},{12,8},{1,5},{5,1},{9,13},{13,9},{2,6},{6,2},{1... | collective-permute-start | bytes 786440 | tf_op jit(solution)/shard_map/ppermute | solution.py:17
  221.2 9.2 %collective-permute-start.24 = (bf16[512,256]{1,0:T(8,128)(2,1)S(1)}, bf16[512,256]{1,0:T(8,128)(2,1)S(1)}, u32[]{:S(2)}, u32[]{:S(2)}) collective-permute-start(bf16[512,256]{1,0:T(8,128)(2,1)S(1)} %attend.4), channel_id=1, source_target_pairs={{0,16},{16,0},{1,17},{17,1},{2,18},{18,2},{3,19},{19,3},{4,20},{20... | collective-permute-start | bytes 786440 | tf_op jit(solution)/shard_map/ppermute | solution.py:17
  221.8 14.3 %collective-permute-start.42 = (bf16[512,256]{1,0:T(8,128)(2,1)S(1)}, bf16[512,256]{1,0:T(8,128)(2,1)S(1)}, u32[]{:S(2)}, u32[]{:S(2)}) collective-permute-start(bf16[512,256]{1,0:T(8,128)(2,1)S(1)} %attend.7), channel_id=1, source_target_pairs={{0,16},{16,0},{1,17},{17,1},{2,18},{18,2},{3,19},{19,3},{4,20},{20... | collective-permute-start | bytes 786440 | tf_op jit(solution)/shard_map/ppermute | solution.py:17
  223.3 18.4 %collective-permute-start.36 = (bf16[512,256]{1,0:T(8,128)(2,1)S(1)}, bf16[512,256]{1,0:T(8,128)(2,1)S(1)}, u32[]{:S(2)}, u32[]{:S(2)}) collective-permute-start(bf16[512,256]{1,0:T(8,128)(2,1)S(1)} %attend.6), channel_id=1, source_target_pairs={{0,16},{16,0},{1,17},{17,1},{2,18},{18,2},{3,19},{19,3},{4,20},{20... | collective-permute-start | bytes 786440 | tf_op jit(solution)/shard_map/ppermute | solution.py:17
  223.9 21.3 %collective-permute-start.30 = (bf16[512,256]{1,0:T(8,128)(2,1)S(1)}, bf16[512,256]{1,0:T(8,128)(2,1)S(1)}, u32[]{:S(2)}, u32[]{:S(2)}) collective-permute-start(bf16[512,256]{1,0:T(8,128)(2,1)S(1)} %attend.5), channel_id=1, source_target_pairs={{0,16},{16,0},{1,17},{17,1},{2,18},{18,2},{3,19},{19,3},{4,20},{20... | collective-permute-start | bytes 786440 | tf_op jit(solution)/shard_map/ppermute | solution.py:17
  (16 other events, 96.1 us)

commit v2 on v1

--- a/solution.py
+++ b/solution.py
@@ -27,10 +27,6 @@
 NEAR = pl.BlockSpec(memory_space=pltpu.VMEM)
 ANY = pl.BlockSpec(memory_space=pl.ANY)
 ALONE = pltpu.CompilerParams(vmem_limit_bytes=62 << 20)
-
-
-def whole(shape):
-    return pl.BlockSpec(shape, lambda i: (0,) * len(shape))
 
 
 def limit(held):
@@ -241,7 +237,7 @@
     return out if join else out[0]
 
 
-def attend_kernel(count, heads, skip, scalars, q_ref, kv_ref, o_ref, keys, values):
+def attend_kernel(count, heads, skip, scalars, q_ref, kv_ref, o_ref, keys, turned, values):
     me, length = scalars[0], scalars[1]
     seqlen = keys.shape[0]
     block = seqlen // count
@@ -249,21 +245,21 @@
     for b in range(count):
         keys[b * block : (b + 1) * block, :] = kv_ref[pl.ds(starts[b], block), :HD]
         values[b * block : (b + 1) * block, :] = kv_ref[pl.ds(starts[b], block), HD : 2 * HD]
+    turned[...] = keys[...].T
     for b in range(count):
         reach = (b + 1) * block
         query = jnp.concatenate(
             [q_ref[pl.ds(starts[b], block), skip + h * HD : skip + (h + 1) * HD] for h in range(heads)], axis=0
         )
-        scores = lax.dot_general(
-            query, keys[:reach, :], (((1,), (1,)), ((), ())), preferred_element_type=F32
-        ) * (1.0 / math.sqrt(HD))
+        scores = jnp.dot(query, turned[:, :reach], preferred_element_type=F32)
         places = b * block + lax.rem(lax.broadcasted_iota(jnp.int32, (heads * block, 1), 0), block)
         last = jnp.minimum(places, length - 1)
         allowed = lax.broadcasted_iota(jnp.int32, (heads * block, reach), 1) <= last
         scores = jnp.where(allowed, scores, jnp.float32(-1e30))
-        expo = jnp.exp(scores - jnp.max(scores, axis=-1, keepdims=True))
-        probs = (expo * (1.0 / jnp.sum(expo, axis=-1, keepdims=True))).astype(BF16)
-        result = jnp.dot(probs, values[:reach, :], preferred_element_type=F32)
+        scale = math.log2(math.e) / math.sqrt(HD)
+        expo = jnp.exp2((scores - jnp.max(scores, axis=-1, keepdims=True)) * scale)
+        result = jnp.dot(expo.astype(BF16), values[:reach, :], preferred_element_type=F32)
+        result = result * (1.0 / jnp.sum(expo, axis=-1, keepdims=True))
         result = jnp.where(places < length, result, 0.0).astype(BF16)
         for h in range(heads):
             o_ref[b * block : reach, h * HD : (h + 1) * HD] = result[h * block : (h + 1) * block]
@@ -274,12 +270,11 @@
     return pl.pallas_call(
         functools.partial(attend_kernel, count, heads, skip),
         out_shape=jax.ShapeDtypeStruct((seqlen, heads * HD), BF16),
-        grid=(1,),
-        in_specs=[SMEM, whole(query.shape), pl.BlockSpec((seqlen, 2 * HD), lambda i: (0, 0))],
-        out_specs=whole((seqlen, heads * HD)),
-        scratch_shapes=[pltpu.VMEM((seqlen, HD), BF16)] * 2,
+        in_specs=[SMEM, NEAR, NEAR],
+        out_specs=NEAR,
+        scratch_shapes=[pltpu.VMEM(shape, BF16) for shape in ((seqlen, HD), (HD, seqlen), (seqlen, HD))],
         cost_estimate=cost(4 * seqlen * seqlen * HD * heads, 4 * seqlen * HD * heads, seqlen * seqlen * heads),
-        compiler_params=limit(12 * seqlen * (query.shape[1] + seqlen * heads)),
+        compiler_params=limit(4 * seqlen * (query.shape[1] + seqlen * heads)),
         name="attend",
     )(scalars, query, keyval)
 
@@ -359,7 +354,8 @@
             keyval = total
         else:
             s1 = inward(project([tokens[3], tokens[2]], w))
-            s2 = inner(project([tokens[2], tokens[3]], w, [(s1, 0, False)]))
+            value = project([tokens[2], tokens[3]], w, [(s1, 0, False)])
+            s2 = inner(value)
             s3 = outer(project([tokens[1]], w, [(s2, 0, True)]))
             total = project([tokens[0]], w, [(s3, 0, False), (s2, seqlen, True)])
         result = attend(count, scalars, total, 0 if g else kv_width, GROUP_HEADS[g], keyval)

time: 247 us -> 246 us (level)
  transfers between devices with their start and end apart: 43 -> 43, of which waited for: 21 -> 21; matrix products, arithmetic and copies ran while one was open for 1% -> 1% of each run, Pallas kernels for 17% -> 16%
where the time goes in v2:
time: 246 us
  waiting for transfers between devices  127 us (52%)
  starting transfers between devices  62.7 us (25%)
  Pallas kernels  47.5 us (19%)
  local copies, waits for them, and re-layouts  6.14 us (2%)
    ppermute x31, waiting for transfers between devices, swap(): lax.ppermute(value, axis, [(i, i ^ bits) for i in range(lax.axis_size(axi...  102 us
    ppermute x31, starting transfers between devices, swap(): lax.ppermute(value, axis, [(i, i ^ bits) for i in range(lax.axis_size(axi...  33.2 us
    pallas_call x19, Pallas kernels, project(): pl.pallas_call(functools.partial(project_kernel, [len(group) for group in...  27.7 us
    ppermute x7, waiting for transfers between devices, inward(): return lax.ppermute(value, 'dp', pairs)  25.3 us
    ppermute x7, starting transfers between devices, inward(): return lax.ppermute(value, 'dp', pairs)  22.1 us
    ppermute x5, starting transfers between devices, inner(): return lax.ppermute(value, ('pool', 'dp'), pairs)  7.52 us
    pallas_call x4, Pallas kernels, attend(): pl.pallas_call(functools.partial(attend_kernel, count, heads, skip), out_...  6.82 us
    unnamed x42, local copies, waits for them, and re-layouts  5.47 us
  transfers between devices with their start and end apart: 43, of which 21 were waited for; matrix products, arithmetic and copies ran while one was open for 1% of the time, Pallas kernels for 16%

profile of v2, /device:TPU:0, one launch (start us, length us, event | category | flops | bytes accessed | tf_op | source)
XLA Modules:
  0.0 245.7 jit_solution(9951675803669824307)
XLA Ops:
  0.0 4.2 %cut.1 = (bf16[512,256]{1,0:T(8,128)(2,1)}, bf16[512,256]{1,0:T(8,128)(2,1)}, bf16[512,256]{1,0:T(8,128)(2,1)}, bf16[512,256]{1,0:T(8,128)(2,1)}, bf16[512,256]{...) custom-call(bf16[512,4096]{1,0:T(8,128)(2,1)} %bitcast.7, ...), custom_call_target="tpu_custom_call" | custom-call | bytes 8388608 | tf_op jit(solution)/shard_map/cut/pallas_call | solution.py:92
  4.7 2.6 %collective-permute-start.25 = (bf16[512,256]{1,0:T(8,128)(2,1)}, bf16[512,256]{1,0:T(8,128)(2,1)S(1)}, u32[]{:S(2)}, u32[]{:S(2)}) collective-permute-start(bf16[512,256]{1,0:T(8,128)(2,1)} %get-tuple-element.43), channel_id=1, source_target_pairs={{0,2},{1,3},{2,0},{3,1},{4,6},{5,7},{6,4},{7,5},{8,10},{9,11},{10,... | collective-permute-start | bytes 786440 | tf_op jit(solution)/shard_map/ppermute | solution.py:17
  7.3 4.6 %begin.1 = (bf16[128,2048]{1,0:T(8,128)(2,1)}, bf16[128,2048]{1,0:T(8,128)(2,1)}, bf16[128,2048]{1,0:T(8,128)(2,1)}, bf16[128,2048]{1,0:T(8,128)(2,1)}, bf16[512...) custom-call(bf16[128,8192]{1,0:T(8,128)(2,1)} %bitcast.11, bf16[2,8192]{1,0:T(2,128)(2,1)} %gain_ref.1, ...), custom_call_target="tpu_custom_call" | custom-call | flops 4194304 | bytes 6291456 | tf_op jit(solution)/shard_map/begin/pallas_call | solution.py:172
  12.0 3.7 %collective-permute-start.15 = (bf16[128,2048]{1,0:T(8,128)(2,1)}, bf16[128,2048]{1,0:T(8,128)(2,1)S(1)}, u32[]{:S(2)}, u32[]{:S(2)}) collective-permute-start(bf16[128,2048]{1,0:T(8,128)(2,1)} %get-tuple-element.37), channel_id=1, source_target_pairs={{0,12},{4,8},{8,4},{12,0},{1,13},{5,9},{9,5},{13,1},{2,14},{6,10},... | collective-permute-start | bytes 1572872 | tf_op jit(solution)/shard_map/ppermute | solution.py:17
  15.7 1.5 collective-permute-start.31
  17.2 7.3 %collective-permute-done.26.refs_3_ = bf16[512,256]{1,0:T(8,128)(2,1)S(1)} collective-permute-done((bf16[512,256]{1,0:T(8,128)(2,1)}, bf16[512,256]{1,0:T(8,128)(2,1)S(1)}, u32[]{:S(2)}, u32[]{:S(2)}) %collective-permute-start.26) | collective-permute-done | bytes 262176 | tf_op jit(solution)/shard_map/ppermute | solution.py:17
  24.8 5.4 %collective-permute-done.31.refs_2_ = bf16[512,256]{1,0:T(8,128)(2,1)S(1)} collective-permute-done((bf16[512,256]{1,0:T(8,128)(2,1)}, bf16[512,256]{1,0:T(8,128)(2,1)S(1)}, u32[]{:S(2)}, u32[]{:S(2)}) %collective-permute-start.31) | collective-permute-done | bytes 262176 | tf_op jit(solution)/shard_map/ppermute | solution.py:17
  30.7 1.5 collective-permute-start.17
  32.2 3.5 %collective-permute-done.32.refs_3_ = bf16[512,256]{1,0:T(8,128)(2,1)S(1)} collective-permute-done((bf16[512,256]{1,0:T(8,128)(2,1)S(1)}, bf16[512,256]{1,0:T(8,128)(2,1)S(1)}, u32[]{:S(2)}, u32[]{:S(2)}) %collective-permute-start.32) | collective-permute-done | bytes 262176 | tf_op jit(solution)/shard_map/ppermute | solution.py:17
  35.9 25.1 %collective-permute-done.11.refs_0_ = bf16[128,2048]{1,0:T(8,128)(2,1)S(1)} collective-permute-done((bf16[128,2048]{1,0:T(8,128)(2,1)}, bf16[128,2048]{1,0:T(8,128)(2,1)S(1)}, u32[]{:S(2)}, u32[]{:S(2)}) %collective-permute-start.11) | collective-permute-done | bytes 524320 | tf_op jit(solution)/shard_map/ppermute | solution.py:17
  62.0 7.4 %collective-permute-done.5.refs_3_ = bf16[512,512]{1,0:T(8,128)(2,1)S(1)} collective-permute-done((bf16[512,512]{1,0:T(8,128)(2,1)}, bf16[512,512]{1,0:T(8,128)(2,1)S(1)}, u32[]{:S(2)}, u32[]{:S(2)}) %collective-permute-start.5) | collective-permute-done | bytes 524320 | tf_op jit(solution)/shard_map/ppermute | solution.py:17
  69.4 5.9 %collective-permute-start.6 = (bf16[128,2048]{1,0:T(8,128)(2,1)}, bf16[128,2048]{1,0:T(8,128)(2,1)S(1)}, u32[]{:S(2)}, u32[]{:S(2)}) collective-permute-start(bf16[128,2048]{1,0:T(8,128)(2,1)} %get-tuple-element.32), channel_id=1, source_target_pairs={{0,4},{4,0},{8,12},{12,8},{1,5},{5,1},{9,13},{13,9},{2,6},{6,2},{1... | collective-permute-start | bytes 1572872 | tf_op jit(solution)/shard_map/ppermute | solution.py:17
  75.3 5.4 %collective-permute-done.13.refs_2_ = bf16[128,2048]{1,0:T(8,128)(2,1)S(1)} collective-permute-done((bf16[128,2048]{1,0:T(8,128)(2,1)S(1)}, bf16[128,2048]{1,0:T(8,128)(2,1)S(1)}, u32[]{:S(2)}, u32[]{:S(2)}) %collective-permute-start.13) | collective-permute-done | bytes 524320 | tf_op jit(solution)/shard_map/ppermute | solution.py:17
  83.0 1.6 collective-permute-start.37
  87.3 2.5 %collective-permute-start.8 = (bf16[128,2048]{1,0:T(8,128)(2,1)S(1)}, bf16[128,2048]{1,0:T(8,128)(2,1)S(1)}, u32[]{:S(2)}, u32[]{:S(2)}) collective-permute-start(bf16[128,2048]{1,0:T(8,128)(2,1)S(1)} %collective-permute-done.6.refs_0_), channel_id=1, source_target_pairs={{0,2},{1,3},{2,0},{3,1},{4,6},{5,7},{6,4},{7,5},{8,10},{9,11},{10,... | collective-permute-start | bytes 1572872 | tf_op jit(solution)/shard_map/ppermute | solution.py:17
  89.8 3.8 %collective-permute-start.19 = (bf16[512,512]{1,0:T(8,128)(2,1)S(1)}, bf16[512,512]{1,0:T(8,128)(2,1)S(1)}, u32[]{:S(2)}, u32[]{:S(2)}) collective-permute-start(bf16[512,512]{1,0:T(8,128)(2,1)S(1)} %get-tuple-element.38), channel_id=1, source_target_pairs={{0,4},{12,8},{1,5},{13,9},{2,6},{14,10},{3,7},{15,11},{16,20},{28,... | collective-permute-start | bytes 1572872 | tf_op jit(solution)/shard_map/ppermute | solution.py:330
  96.0 6.9 %collective-permute-done.37.refs_2_ = bf16[512,256]{1,0:T(8,128)(2,1)S(1)} collective-permute-done((bf16[512,256]{1,0:T(8,128)(2,1)S(1)}, bf16[512,256]{1,0:T(8,128)(2,1)S(1)}, u32[]{:S(2)}, u32[]{:S(2)}) %collective-permute-start.37) | collective-permute-done | bytes 262176 | tf_op jit(solution)/shard_map/ppermute | solution.py:17
  104.1 13.8 %collective-permute-done.38.refs_3_ = bf16[512,256]{1,0:T(8,128)(2,1)S(1)} collective-permute-done((bf16[512,256]{1,0:T(8,128)(2,1)S(1)}, bf16[512,256]{1,0:T(8,128)(2,1)S(1)}, u32[]{:S(2)}, u32[]{:S(2)}) %collective-permute-start.38) | collective-permute-done | bytes 262176 | tf_op jit(solution)/shard_map/ppermute | solution.py:17
  117.9 7.1 %collective-permute-start.27 = (bf16[1024,256]{1,0:T(8,128)(2,1)S(1)}, bf16[1024,256]{1,0:T(8,128)(2,1)S(1)}, u32[]{:S(2)}, u32[]{:S(2)}) collective-permute-start(bf16[1024,256]{1,0:T(8,128)(2,1)S(1)} %project.26), channel_id=1, source_target_pairs={{0,4},{12,8},{1,5},{13,9},{2,6},{14,10},{3,7},{15,11},{16,20},{28,... | collective-permute-start | bytes 1572872 | tf_op jit(solution)/shard_map/ppermute | solution.py:330
  131.5 1.5 collective-permute-start.39
  134.3 1.5 collective-permute-start.22
  140.0 8.5 %collective-permute-done.33.refs_3_ = bf16[1024,256]{1,0:T(8,128)(2,1)S(1)} collective-permute-done((bf16[1024,256]{1,0:T(8,128)(2,1)S(1)}, bf16[1024,256]{1,0:T(8,128)(2,1)S(1)}, u32[]{:S(2)}, u32[]{:S(2)}) %collective-permute-start.33) | collective-permute-done | bytes 524320 | tf_op jit(solution)/shard_map/ppermute | solution.py:330
  149.8 1.6 collective-permute-start.28
  151.3 8.4 %collective-permute-done.39.refs_3_ = bf16[1024,256]{1,0:T(8,128)(2,1)S(1)} collective-permute-done((bf16[1024,256]{1,0:T(8,128)(2,1)S(1)}, bf16[1024,256]{1,0:T(8,128)(2,1)S(1)}, u32[]{:S(2)}, u32[]{:S(2)}) %collective-permute-start.39) | collective-permute-done | bytes 524320 | tf_op jit(solution)/shard_map/ppermute | solution.py:330
  161.2 2.1 project.19
  163.4 2.0 project.35
  165.4 5.4 %collective-permute-done.22.refs_2_ = bf16[512,512]{1,0:T(8,128)(2,1)S(1)} collective-permute-done((bf16[512,512]{1,0:T(8,128)(2,1)S(1)}, bf16[512,512]{1,0:T(8,128)(2,1)S(1)}, u32[]{:S(2)}, u32[]{:S(2)}) %collective-permute-start.22) | collective-permute-done | bytes 524320 | tf_op jit(solution)/shard_map/ppermute | solution.py:330
  172.3 2.0 project.24
  174.3 2.1 project.23
  177.2 5.3 %collective-permute-start.10 = (bf16[512,512]{1,0:T(8,128)(2,1)}, bf16[512,512]{1,0:T(8,128)(2,1)}, u32[]{:S(2)}, u32[]{:S(2)}) collective-permute-start(bf16[512,512]{1,0:T(8,128)(2,1)} %get-tuple-element.33), channel_id=1, source_target_pairs={{0,4},{12,8},{1,5},{13,9},{2,6},{14,10},{3,7},{15,11},{16,20},{28,... | collective-permute-start | bytes 1572872 | tf_op jit(solution)/shard_map/ppermute | solution.py:330
  184.7 1.5 collective-permute-start.21
  186.9 1.6 copy-done.4
  192.3 3.3 %collective-permute-start.29 = (bf16[512,256]{1,0:T(8,128)(2,1)S(1)}, bf16[512,256]{1,0:T(8,128)(2,1)S(1)}, u32[]{:S(2)}, u32[]{:S(2)}) collective-permute-start(bf16[512,256]{1,0:T(8,128)(2,1)S(1)} %project.28), channel_id=1, source_target_pairs={{0,4},{4,0},{8,12},{12,8},{1,5},{5,1},{9,13},{13,9},{2,6},{6,2},{1... | collective-permute-start | bytes 786440 | tf_op jit(solution)/shard_map/ppermute | solution.py:17
  196.5 1.8 project.36
  198.2 2.0 collective-permute-start.41
  201.8 3.0 %project.25 = (bf16[512,512]{1,0:T(8,128)(2,1)S(1)}, bf16[512,2048]{1,0:T(8,128)(2,1)S(1)}) custom-call(bf16[128,2048]{1,0:T(8,128)(2,1)S(1)} %copy-done.15, bf16[128,2048]{1,0:T(8,128)(2,1)S(1)} %copy-done.17, bf16[128,2048]{1,0:T(8,128)(2,1)} %collective-permute-done.1.refs_2_, bf16[128,2048]{1,0:T(8,128)(2,1)} %collective-permute-done.2.refs_3_, ...), custom_call_target="tpu_custom_call" | custom-call | flops 1073741824 | bytes 4718592 | tf_op jit(solution)/shard_map/project/pallas_call | solution.py:226
  204.8 1.7 attend.4
  208.0 1.7 attend.5
  209.7 3.2 %collective-permute-done.35.refs_2_ = bf16[512,256]{1,0:T(8,128)(2,1)S(1)} collective-permute-done((bf16[512,256]{1,0:T(8,128)(2,1)S(1)}, bf16[512,256]{1,0:T(8,128)(2,1)S(1)}, u32[]{:S(2)}, u32[]{:S(2)}) %collective-permute-start.35) | collective-permute-done | bytes 262176 | tf_op jit(solution)/shard_map/ppermute | solution.py:17
  213.6 1.7 attend.6
  215.3 1.9 collective-permute-done.41.refs_2_
  217.2 1.8 project.37.q_ref
  218.9 1.7 attend.7
  221.3 1.5 collective-permute-start.42
  224.8 5.1 %collective-permute-done.24 = bf16[512,256]{1,0:T(8,128)(2,1)S(1)} collective-permute-done((bf16[512,256]{1,0:T(8,128)(2,1)S(1)}, bf16[512,256]{1,0:T(8,128)(2,1)S(1)}, u32[]{:S(2)}, u32[]{:S(2)}) %collective-permute-start.24) | collective-permute-done | bytes 262176 | tf_op jit(solution)/shard_map/ppermute | solution.py:17
  229.9 5.6 %collective-permute-done.42 = bf16[512,256]{1,0:T(8,128)(2,1)S(1)} collective-permute-done((bf16[512,256]{1,0:T(8,128)(2,1)S(1)}, bf16[512,256]{1,0:T(8,128)(2,1)S(1)}, u32[]{:S(2)}, u32[]{:S(2)}) %collective-permute-start.42) | collective-permute-done | bytes 262176 | tf_op jit(solution)/shard_map/ppermute | solution.py:17
  235.5 5.6 %collective-permute-done.36 = bf16[512,256]{1,0:T(8,128)(2,1)S(1)} collective-permute-done((bf16[512,256]{1,0:T(8,128)(2,1)S(1)}, bf16[512,256]{1,0:T(8,128)(2,1)S(1)}, u32[]{:S(2)}, u32[]{:S(2)}) %collective-permute-start.36) | collective-permute-done | bytes 262176 | tf_op jit(solution)/shard_map/ppermute | solution.py:17
  241.1 3.5 %collective-permute-done.30 = bf16[512,256]{1,0:T(8,128)(2,1)S(1)} collective-permute-done((bf16[512,256]{1,0:T(8,128)(2,1)S(1)}, bf16[512,256]{1,0:T(8,128)(2,1)S(1)}, u32[]{:S(2)}, u32[]{:S(2)}) %collective-permute-start.30) | collective-permute-done | bytes 262176 | tf_op jit(solution)/shard_map/ppermute | solution.py:17
  (112 shorter events, 43.1 us)
Async XLA Ops:
  0.0 186.3 %copy-start = (s32[2,1]{0,1:T(1,128)S(1)}, s32[2,1]{0,1:T(1,128)}, u32[]{:S(2)}) copy-start(s32[2,1]{0,1:T(1,128)} %param.6) | copy-start | bytes 28
  4.2 76.5 %collective-permute-start.3 = (bf16[512,1280]{1,0:T(8,128)(2,1)}, bf16[512,1280]{1,0:T(8,128)(2,1)}, u32[]{:S(2)}, u32[]{:S(2)}) collective-permute-start(bf16[512,1280]{1,0:T(8,128)(2,1)} %get-tuple-element.29), channel_id=1, source_target_pairs={{0,1},{1,0},{2,3},{3,2},{4,5},{5,4},{6,7},{7,6},{8,9},{9,8},{10,11... | collective-permute-start | bytes 3932168 | tf_op jit(solution)/shard_map/ppermute | solution.py:17
  4.7 10.9 %collective-permute-start.25 = (bf16[512,256]{1,0:T(8,128)(2,1)}, bf16[512,256]{1,0:T(8,128)(2,1)S(1)}, u32[]{:S(2)}, u32[]{:S(2)}) collective-permute-start(bf16[512,256]{1,0:T(8,128)(2,1)} %get-tuple-element.43), channel_id=1, source_target_pairs={{0,2},{1,3},{2,0},{3,1},{4,6},{5,7},{6,4},{7,5},{8,10},{9,11},{10,... | collective-permute-start | bytes 786440 | tf_op jit(solution)/shard_map/ppermute | solution.py:17
  7.3 73.8 %copy-start.9 = (bf16[512,1280]{1,0:T(8,128)(2,1)S(1)}, bf16[512,1280]{1,0:T(8,128)(2,1)}, u32[]{:S(2)}) copy-start(bf16[512,1280]{1,0:T(8,128)(2,1)} %get-tuple-element.28.refs_0_) | copy-start | bytes 3932164
  12.0 18.7 %collective-permute-start.15 = (bf16[128,2048]{1,0:T(8,128)(2,1)}, bf16[128,2048]{1,0:T(8,128)(2,1)S(1)}, u32[]{:S(2)}, u32[]{:S(2)}) collective-permute-start(bf16[128,2048]{1,0:T(8,128)(2,1)} %get-tuple-element.37), channel_id=1, source_target_pairs={{0,12},{4,8},{8,4},{12,0},{1,13},{5,9},{9,5},{13,1},{2,14},{6,10},... | collective-permute-start | bytes 1572872 | tf_op jit(solution)/shard_map/ppermute | solution.py:17
  15.7 8.8 %collective-permute-start.26 = (bf16[512,256]{1,0:T(8,128)(2,1)}, bf16[512,256]{1,0:T(8,128)(2,1)S(1)}, u32[]{:S(2)}, u32[]{:S(2)}) collective-permute-start(bf16[512,256]{1,0:T(8,128)(2,1)} %get-tuple-element.44), channel_id=1, source_target_pairs={{0,3},{1,2},{2,1},{3,0},{4,7},{5,6},{6,5},{7,4},{8,11},{9,10},{10,... | collective-permute-start | bytes 786440 | tf_op jit(solution)/shard_map/ppermute | solution.py:17
  15.7 45.3 %collective-permute-start.11 = (bf16[128,2048]{1,0:T(8,128)(2,1)}, bf16[128,2048]{1,0:T(8,128)(2,1)S(1)}, u32[]{:S(2)}, u32[]{:S(2)}) collective-permute-start(bf16[128,2048]{1,0:T(8,128)(2,1)} %get-tuple-element.35), channel_id=1, source_target_pairs={{0,8},{4,12},{8,0},{12,4},{1,9},{5,13},{9,1},{13,5},{2,10},{6,14},... | collective-permute-start | bytes 1572872 | tf_op jit(solution)/shard_map/ppermute | solution.py:17
  15.7 14.5 %collective-permute-start.31 = (bf16[512,256]{1,0:T(8,128)(2,1)}, bf16[512,256]{1,0:T(8,128)(2,1)S(1)}, u32[]{:S(2)}, u32[]{:S(2)}) collective-permute-start(bf16[512,256]{1,0:T(8,128)(2,1)} %get-tuple-element.45), channel_id=1, source_target_pairs={{0,2},{1,3},{2,0},{3,1},{4,6},{5,7},{6,4},{7,5},{8,10},{9,11},{10,... | collective-permute-start | bytes 786440 | tf_op jit(solution)/shard_map/ppermute | solution.py:17
  24.4 11.2 %collective-permute-start.32 = (bf16[512,256]{1,0:T(8,128)(2,1)S(1)}, bf16[512,256]{1,0:T(8,128)(2,1)S(1)}, u32[]{:S(2)}, u32[]{:S(2)}) collective-permute-start(bf16[512,256]{1,0:T(8,128)(2,1)S(1)} %copy-done.20), channel_id=1, source_target_pairs={{0,3},{1,2},{2,1},{3,0},{4,7},{5,6},{6,5},{7,4},{8,11},{9,10},{10,... | collective-permute-start | bytes 786440 | tf_op jit(solution)/shard_map/ppermute | solution.py:17
  30.1 31.3 %collective-permute-start.4 = (bf16[512,512]{1,0:T(8,128)(2,1)}, bf16[512,512]{1,0:T(8,128)(2,1)S(1)}, u32[]{:S(2)}, u32[]{:S(2)}) collective-permute-start(bf16[512,512]{1,0:T(8,128)(2,1)} %get-tuple-element.30), channel_id=1, source_target_pairs={{0,2},{1,3},{2,0},{3,1},{4,6},{5,7},{6,4},{7,5},{8,10},{9,11},{10,... | collective-permute-start | bytes 1572872 | tf_op jit(solution)/shard_map/ppermute | solution.py:17
  30.7 30.8 %collective-permute-start.17 = (bf16[128,2048]{1,0:T(8,128)(2,1)S(1)}, bf16[128,2048]{1,0:T(8,128)(2,1)S(1)}, u32[]{:S(2)}, u32[]{:S(2)}) collective-permute-start(bf16[128,2048]{1,0:T(8,128)(2,1)S(1)} %collective-permute-done.15.refs_0_), channel_id=1, source_target_pairs={{0,2},{1,3},{2,0},{3,1},{4,6},{5,7},{6,4},{7,5},{8,10},{9,11},{10,... | collective-permute-start | bytes 1572872 | tf_op jit(solution)/shard_map/ppermute | solution.py:17
  35.7 33.7 %collective-permute-start.5 = (bf16[512,512]{1,0:T(8,128)(2,1)}, bf16[512,512]{1,0:T(8,128)(2,1)S(1)}, u32[]{:S(2)}, u32[]{:S(2)}) collective-permute-start(bf16[512,512]{1,0:T(8,128)(2,1)} %get-tuple-element.31), channel_id=1, source_target_pairs={{0,3},{1,2},{2,1},{3,0},{4,7},{5,6},{6,5},{7,4},{8,11},{9,10},{10,... | collective-permute-start | bytes 1572872 | tf_op jit(solution)/shard_map/ppermute | solution.py:17
  61.0 19.7 %collective-permute-start.13 = (bf16[128,2048]{1,0:T(8,128)(2,1)S(1)}, bf16[128,2048]{1,0:T(8,128)(2,1)S(1)}, u32[]{:S(2)}, u32[]{:S(2)}) collective-permute-start(bf16[128,2048]{1,0:T(8,128)(2,1)S(1)} %collective-permute-done.11.refs_0_), channel_id=1, source_target_pairs={{0,2},{1,3},{2,0},{3,1},{4,6},{5,7},{6,4},{7,5},{8,10},{9,11},{10,... | collective-permute-start | bytes 1572872 | tf_op jit(solution)/shard_map/ppermute | solution.py:17
  61.5 20.9 %collective-permute-start.16 = (bf16[128,2048]{1,0:T(8,128)(2,1)S(1)}, bf16[128,2048]{1,0:T(8,128)(2,1)S(1)}, u32[]{:S(2)}, u32[]{:S(2)}) collective-permute-start(bf16[128,2048]{1,0:T(8,128)(2,1)S(1)} %collective-permute-done.15.refs_0_), channel_id=1, source_target_pairs={{0,1},{1,0},{2,3},{3,2},{4,5},{5,4},{6,7},{7,6},{8,9},{9,8},{10,11... | collective-permute-start | bytes 1572872 | tf_op jit(solution)/shard_map/ppermute | solution.py:17
  61.5 21.5 %collective-permute-start.18 = (bf16[128,2048]{1,0:T(8,128)(2,1)S(1)}, bf16[128,2048]{1,0:T(8,128)(2,1)S(1)}, u32[]{:S(2)}, u32[]{:S(2)}) collective-permute-start(bf16[128,2048]{1,0:T(8,128)(2,1)S(1)} %collective-permute-done.17.refs_2_), channel_id=1, source_target_pairs={{0,1},{1,0},{2,3},{3,2},{4,5},{5,4},{6,7},{7,6},{8,9},{9,8},{10,11... | collective-permute-start | bytes 1572872 | tf_op jit(solution)/shard_map/ppermute | solution.py:17
  69.4 17.9 %collective-permute-start.6 = (bf16[128,2048]{1,0:T(8,128)(2,1)}, bf16[128,2048]{1,0:T(8,128)(2,1)S(1)}, u32[]{:S(2)}, u32[]{:S(2)}) collective-permute-start(bf16[128,2048]{1,0:T(8,128)(2,1)} %get-tuple-element.32), channel_id=1, source_target_pairs={{0,4},{4,0},{8,12},{12,8},{1,5},{5,1},{9,13},{13,9},{2,6},{6,2},{1... | collective-permute-start | bytes 1572872 | tf_op jit(solution)/shard_map/ppermute | solution.py:17
  80.6 9.1 %collective-permute-start.12 = (bf16[128,2048]{1,0:T(8,128)(2,1)S(1)}, bf16[128,2048]{1,0:T(8,128)(2,1)S(1)}, u32[]{:S(2)}, u32[]{:S(2)}) collective-permute-start(bf16[128,2048]{1,0:T(8,128)(2,1)S(1)} %collective-permute-done.11.refs_0_), channel_id=1, source_target_pairs={{0,1},{1,0},{2,3},{3,2},{4,5},{5,4},{6,7},{7,6},{8,9},{9,8},{10,11... | collective-permute-start | bytes 1572872 | tf_op jit(solution)/shard_map/ppermute | solution.py:17
  80.7 12.9 %collective-permute-start.14 = (bf16[128,2048]{1,0:T(8,128)(2,1)S(1)}, bf16[128,2048]{1,0:T(8,128)(2,1)S(1)}, u32[]{:S(2)}, u32[]{:S(2)}) collective-permute-start(bf16[128,2048]{1,0:T(8,128)(2,1)S(1)} %collective-permute-done.13.refs_2_), channel_id=1, source_target_pairs={{0,1},{1,0},{2,3},{3,2},{4,5},{5,4},{6,7},{7,6},{8,9},{9,8},{10,11... | collective-permute-start | bytes 1572872 | tf_op jit(solution)/shard_map/ppermute | solution.py:17
  82.4 92.0 %copy-start.1 = (bf16[2048,512]{1,0:T(8,128)(2,1)}, bf16[2048,512]{1,0:T(8,128)(2,1)S(1)}, u32[]{:S(2)}) copy-start(bf16[2048,512]{1,0:T(8,128)(2,1)S(1)} %stack.12.refs_4_.refs_1_) | copy-start | bytes 6291460
  82.4 45.9 %collective-permute-start.1 = (bf16[128,2048]{1,0:T(8,128)(2,1)S(1)}, bf16[128,2048]{1,0:T(8,128)(2,1)}, u32[]{:S(2)}, u32[]{:S(2)}) collective-permute-start(bf16[128,2048]{1,0:T(8,128)(2,1)S(1)} %copy-done.14), channel_id=1, source_target_pairs={{0,2},{1,3},{2,0},{3,1},{4,6},{5,7},{6,4},{7,5},{8,10},{9,11},{10,... | collective-permute-start | bytes 1572872 | tf_op jit(solution)/shard_map/ppermute | solution.py:17
  83.0 19.9 %collective-permute-start.37 = (bf16[512,256]{1,0:T(8,128)(2,1)S(1)}, bf16[512,256]{1,0:T(8,128)(2,1)S(1)}, u32[]{:S(2)}, u32[]{:S(2)}) collective-permute-start(bf16[512,256]{1,0:T(8,128)(2,1)S(1)} %copy-done.19), channel_id=1, source_target_pairs={{0,2},{1,3},{2,0},{3,1},{4,6},{5,7},{6,4},{7,5},{8,10},{9,11},{10,... | collective-permute-start | bytes 786440 | tf_op jit(solution)/shard_map/ppermute | solution.py:17
  87.3 43.7 %collective-permute-start.8 = (bf16[128,2048]{1,0:T(8,128)(2,1)S(1)}, bf16[128,2048]{1,0:T(8,128)(2,1)S(1)}, u32[]{:S(2)}, u32[]{:S(2)}) collective-permute-start(bf16[128,2048]{1,0:T(8,128)(2,1)S(1)} %collective-permute-done.6.refs_0_), channel_id=1, source_target_pairs={{0,2},{1,3},{2,0},{3,1},{4,6},{5,7},{6,4},{7,5},{8,10},{9,11},{10,... | collective-permute-start | bytes 1572872 | tf_op jit(solution)/shard_map/ppermute | solution.py:17
  89.8 41.7 %collective-permute-start.19 = (bf16[512,512]{1,0:T(8,128)(2,1)S(1)}, bf16[512,512]{1,0:T(8,128)(2,1)S(1)}, u32[]{:S(2)}, u32[]{:S(2)}) collective-permute-start(bf16[512,512]{1,0:T(8,128)(2,1)S(1)} %get-tuple-element.38), channel_id=1, source_target_pairs={{0,4},{12,8},{1,5},{13,9},{2,6},{14,10},{3,7},{15,11},{16,20},{28,... | collective-permute-start | bytes 1572872 | tf_op jit(solution)/shard_map/ppermute | solution.py:330
  93.6 24.3 %collective-permute-start.38 = (bf16[512,256]{1,0:T(8,128)(2,1)S(1)}, bf16[512,256]{1,0:T(8,128)(2,1)S(1)}, u32[]{:S(2)}, u32[]{:S(2)}) collective-permute-start(bf16[512,256]{1,0:T(8,128)(2,1)S(1)} %copy-done.18), channel_id=1, source_target_pairs={{0,3},{1,2},{2,1},{3,0},{4,7},{5,6},{6,5},{7,4},{8,11},{9,10},{10,... | collective-permute-start | bytes 786440 | tf_op jit(solution)/shard_map/ppermute | solution.py:17
  102.9 31.4 %collective-permute-start.7 = (bf16[128,2048]{1,0:T(8,128)(2,1)S(1)}, bf16[128,2048]{1,0:T(8,128)(2,1)S(1)}, u32[]{:S(2)}, u32[]{:S(2)}) collective-permute-start(bf16[128,2048]{1,0:T(8,128)(2,1)S(1)} %collective-permute-done.6.refs_0_), channel_id=1, source_target_pairs={{0,1},{1,0},{2,3},{3,2},{4,5},{5,4},{6,7},{7,6},{8,9},{9,8},{10,11... | collective-permute-start | bytes 1572872 | tf_op jit(solution)/shard_map/ppermute | solution.py:17
  102.9 22.1 %copy-start.10 = (bf16[512,1280]{1,0:T(8,128)(2,1)S(1)}, bf16[512,1280]{1,0:T(8,128)(2,1)}, u32[]{:S(2)}) copy-start(bf16[512,1280]{1,0:T(8,128)(2,1)} %get-tuple-element.28.refs_0_) | copy-start | bytes 3932164
  117.9 19.4 %collective-permute-start.27 = (bf16[1024,256]{1,0:T(8,128)(2,1)S(1)}, bf16[1024,256]{1,0:T(8,128)(2,1)S(1)}, u32[]{:S(2)}, u32[]{:S(2)}) collective-permute-start(bf16[1024,256]{1,0:T(8,128)(2,1)S(1)} %project.26), channel_id=1, source_target_pairs={{0,4},{12,8},{1,5},{13,9},{2,6},{14,10},{3,7},{15,11},{16,20},{28,... | collective-permute-start | bytes 1572872 | tf_op jit(solution)/shard_map/ppermute | solution.py:330
  127.1 21.4 %copy-start.6 = (bf16[2048,256]{1,0:T(8,128)(2,1)}, bf16[2048,256]{1,0:T(8,128)(2,1)S(1)}, u32[]{:S(2)}) copy-start(bf16[2048,256]{1,0:T(8,128)(2,1)S(1)} %stack.14.refs_2_.refs_1_) | copy-start | bytes 3145732
  128.3 20.2 %collective-permute-start.33 = (bf16[1024,256]{1,0:T(8,128)(2,1)S(1)}, bf16[1024,256]{1,0:T(8,128)(2,1)S(1)}, u32[]{:S(2)}, u32[]{:S(2)}) collective-permute-start(bf16[1024,256]{1,0:T(8,128)(2,1)S(1)} %project.30), channel_id=1, source_target_pairs={{0,4},{12,8},{1,5},{13,9},{2,6},{14,10},{3,7},{15,11},{16,20},{28,... | collective-permute-start | bytes 1572872 | tf_op jit(solution)/shard_map/ppermute | solution.py:330
  130.9 18.8 %collective-permute-start.9 = (bf16[128,2048]{1,0:T(8,128)(2,1)S(1)}, bf16[128,2048]{1,0:T(8,128)(2,1)S(1)}, u32[]{:S(2)}, u32[]{:S(2)}) collective-permute-start(bf16[128,2048]{1,0:T(8,128)(2,1)S(1)} %collective-permute-done.8.refs_2_), channel_id=1, source_target_pairs={{0,1},{1,0},{2,3},{3,2},{4,5},{5,4},{6,7},{7,6},{8,9},{9,8},{10,11... | collective-permute-start | bytes 1572872 | tf_op jit(solution)/shard_map/ppermute | solution.py:17
  131.5 28.3 %collective-permute-start.39 = (bf16[1024,256]{1,0:T(8,128)(2,1)S(1)}, bf16[1024,256]{1,0:T(8,128)(2,1)S(1)}, u32[]{:S(2)}, u32[]{:S(2)}) collective-permute-start(bf16[1024,256]{1,0:T(8,128)(2,1)S(1)} %project.34), channel_id=1, source_target_pairs={{0,4},{12,8},{1,5},{13,9},{2,6},{14,10},{3,7},{15,11},{16,20},{28,... | collective-permute-start | bytes 1572872 | tf_op jit(solution)/shard_map/ppermute | solution.py:330
  134.3 36.5 %collective-permute-start.22 = (bf16[512,512]{1,0:T(8,128)(2,1)S(1)}, bf16[512,512]{1,0:T(8,128)(2,1)S(1)}, u32[]{:S(2)}, u32[]{:S(2)}) collective-permute-start(bf16[512,512]{1,0:T(8,128)(2,1)S(1)} %get-tuple-element.40), channel_id=1, source_target_pairs={{0,4},{12,8},{1,5},{13,9},{2,6},{14,10},{3,7},{15,11},{16,20},{28,... | collective-permute-start | bytes 1572872 | tf_op jit(solution)/shard_map/ppermute | solution.py:330
  137.3 33.5 %collective-permute-start.20 = (bf16[512,512]{1,0:T(8,128)(2,1)S(1)}, bf16[512,512]{1,0:T(8,128)(2,1)S(1)}, u32[]{:S(2)}, u32[]{:S(2)}) collective-permute-start(bf16[512,512]{1,0:T(8,128)(2,1)S(1)} %project.22), channel_id=1, source_target_pairs={{4,8},{8,4},{20,24},{24,20},{0,16},{12,28},{16,0},{28,12},{5,9},{9... | collective-permute-start | bytes 1572872 | tf_op jit(solution)/shard_map/ppermute | solution.py:335
  148.5 27.9 %collective-permute-start = (bf16[128,2048]{1,0:T(8,128)(2,1)S(1)}, bf16[128,2048]{1,0:T(8,128)(2,1)S(1)}, u32[]{:S(2)}, u32[]{:S(2)}) collective-permute-start(bf16[128,2048]{1,0:T(8,128)(2,1)S(1)} %copy-done.14), channel_id=1, source_target_pairs={{0,1},{1,0},{2,3},{3,2},{4,5},{5,4},{6,7},{7,6},{8,9},{9,8},{10,11... | collective-permute-start | bytes 1572872 | tf_op jit(solution)/shard_map/ppermute | solution.py:17
  149.8 32.7 %collective-permute-start.28 = (bf16[1024,256]{1,0:T(8,128)(2,1)S(1)}, bf16[1024,256]{1,0:T(8,128)(2,1)S(1)}, u32[]{:S(2)}, u32[]{:S(2)}) collective-permute-start(bf16[1024,256]{1,0:T(8,128)(2,1)S(1)} %project.27), channel_id=1, source_target_pairs={{4,8},{8,4},{20,24},{24,20},{0,16},{12,28},{16,0},{28,12},{5,9},{9... | collective-permute-start | bytes 1572872 | tf_op jit(solution)/shard_map/ppermute | solution.py:335
  159.7 25.0 %collective-permute-start.34 = (bf16[1024,256]{1,0:T(8,128)(2,1)S(1)}, bf16[1024,256]{1,0:T(8,128)(2,1)S(1)}, u32[]{:S(2)}, u32[]{:S(2)}) collective-permute-start(bf16[1024,256]{1,0:T(8,128)(2,1)S(1)} %project.31), channel_id=1, source_target_pairs={{4,8},{8,4},{20,24},{24,20},{0,16},{12,28},{16,0},{28,12},{5,9},{9... | collective-permute-start | bytes 1572872 | tf_op jit(solution)/shard_map/ppermute | solution.py:335
  170.8 21.5 %collective-permute-start.2 = (bf16[128,2048]{1,0:T(8,128)(2,1)}, bf16[128,2048]{1,0:T(8,128)(2,1)}, u32[]{:S(2)}, u32[]{:S(2)}) collective-permute-start(bf16[128,2048]{1,0:T(8,128)(2,1)} %collective-permute-done.1.refs_2_), channel_id=1, source_target_pairs={{0,1},{1,0},{2,3},{3,2},{4,5},{5,4},{6,7},{7,6},{8,9},{9,8},{10,11... | collective-permute-start | bytes 1572872 | tf_op jit(solution)/shard_map/ppermute | solution.py:17
  170.8 24.8 %collective-permute-start.40 = (bf16[1024,256]{1,0:T(8,128)(2,1)}, bf16[1024,256]{1,0:T(8,128)(2,1)}, u32[]{:S(2)}, u32[]{:S(2)}) collective-permute-start(bf16[1024,256]{1,0:T(8,128)(2,1)} %project.35), channel_id=1, source_target_pairs={{4,8},{8,4},{20,24},{24,20},{0,16},{12,28},{16,0},{28,12},{5,9},{9... | collective-permute-start | bytes 1572872 | tf_op jit(solution)/shard_map/ppermute | solution.py:335
  177.2 21.1 %collective-permute-start.10 = (bf16[512,512]{1,0:T(8,128)(2,1)}, bf16[512,512]{1,0:T(8,128)(2,1)}, u32[]{:S(2)}, u32[]{:S(2)}) collective-permute-start(bf16[512,512]{1,0:T(8,128)(2,1)} %get-tuple-element.33), channel_id=1, source_target_pairs={{0,4},{12,8},{1,5},{13,9},{2,6},{14,10},{3,7},{15,11},{16,20},{28,... | collective-permute-start | bytes 1572872 | tf_op jit(solution)/shard_map/ppermute | solution.py:330
  183.3 17.0 %collective-permute-start.23 = (bf16[512,512]{1,0:T(8,128)(2,1)}, bf16[512,512]{1,0:T(8,128)(2,1)}, u32[]{:S(2)}, u32[]{:S(2)}) collective-permute-start(bf16[512,512]{1,0:T(8,128)(2,1)} %project.24), channel_id=1, source_target_pairs={{4,8},{8,4},{20,24},{24,20},{0,16},{12,28},{16,0},{28,12},{5,9},{9... | collective-permute-start | bytes 1572872 | tf_op jit(solution)/shard_map/ppermute | solution.py:335
  184.7 17.0 %collective-permute-start.21 = (bf16[512,512]{1,0:T(8,128)(2,1)}, bf16[512,512]{1,0:T(8,128)(2,1)}, u32[]{:S(2)}, u32[]{:S(2)}) collective-permute-start(bf16[512,512]{1,0:T(8,128)(2,1)} %project.23), channel_id=1, source_target_pairs={{4,0},{8,12},{5,1},{9,13},{6,2},{10,14},{7,3},{11,15},{20,16},{24,... | collective-permute-start | bytes 1572872 | tf_op jit(solution)/shard_map/ppermute | solution.py:330
  192.3 15.0 %collective-permute-start.29 = (bf16[512,256]{1,0:T(8,128)(2,1)S(1)}, bf16[512,256]{1,0:T(8,128)(2,1)S(1)}, u32[]{:S(2)}, u32[]{:S(2)}) collective-permute-start(bf16[512,256]{1,0:T(8,128)(2,1)S(1)} %project.28), channel_id=1, source_target_pairs={{0,4},{4,0},{8,12},{12,8},{1,5},{5,1},{9,13},{13,9},{2,6},{6,2},{1... | collective-permute-start | bytes 786440 | tf_op jit(solution)/shard_map/ppermute | solution.py:17
  195.6 17.3 %collective-permute-start.35 = (bf16[512,256]{1,0:T(8,128)(2,1)S(1)}, bf16[512,256]{1,0:T(8,128)(2,1)S(1)}, u32[]{:S(2)}, u32[]{:S(2)}) collective-permute-start(bf16[512,256]{1,0:T(8,128)(2,1)S(1)} %project.32), channel_id=1, source_target_pairs={{0,4},{4,0},{8,12},{12,8},{1,5},{5,1},{9,13},{13,9},{2,6},{6,2},{1... | collective-permute-start | bytes 786440 | tf_op jit(solution)/shard_map/ppermute | solution.py:17
  198.2 18.9 %collective-permute-start.41 = (bf16[512,256]{1,0:T(8,128)(2,1)S(1)}, bf16[512,256]{1,0:T(8,128)(2,1)S(1)}, u32[]{:S(2)}, u32[]{:S(2)}) collective-permute-start(bf16[512,256]{1,0:T(8,128)(2,1)S(1)} %project.36), channel_id=1, source_target_pairs={{0,4},{4,0},{8,12},{12,8},{1,5},{5,1},{9,13},{13,9},{2,6},{6,2},{1... | collective-permute-start | bytes 786440 | tf_op jit(solution)/shard_map/ppermute | solution.py:17
  220.7 9.2 %collective-permute-start.24 = (bf16[512,256]{1,0:T(8,128)(2,1)S(1)}, bf16[512,256]{1,0:T(8,128)(2,1)S(1)}, u32[]{:S(2)}, u32[]{:S(2)}) collective-permute-start(bf16[512,256]{1,0:T(8,128)(2,1)S(1)} %attend.4), channel_id=1, source_target_pairs={{0,16},{16,0},{1,17},{17,1},{2,18},{18,2},{3,19},{19,3},{4,20},{20... | collective-permute-start | bytes 786440 | tf_op jit(solution)/shard_map/ppermute | solution.py:17
  221.3 14.3 %collective-permute-start.42 = (bf16[512,256]{1,0:T(8,128)(2,1)S(1)}, bf16[512,256]{1,0:T(8,128)(2,1)S(1)}, u32[]{:S(2)}, u32[]{:S(2)}) collective-permute-start(bf16[512,256]{1,0:T(8,128)(2,1)S(1)} %attend.7), channel_id=1, source_target_pairs={{0,16},{16,0},{1,17},{17,1},{2,18},{18,2},{3,19},{19,3},{4,20},{20... | collective-permute-start | bytes 786440 | tf_op jit(solution)/shard_map/ppermute | solution.py:17
  222.8 18.4 %collective-permute-start.36 = (bf16[512,256]{1,0:T(8,128)(2,1)S(1)}, bf16[512,256]{1,0:T(8,128)(2,1)S(1)}, u32[]{:S(2)}, u32[]{:S(2)}) collective-permute-start(bf16[512,256]{1,0:T(8,128)(2,1)S(1)} %attend.6), channel_id=1, source_target_pairs={{0,16},{16,0},{1,17},{17,1},{2,18},{18,2},{3,19},{19,3},{4,20},{20... | collective-permute-start | bytes 786440 | tf_op jit(solution)/shard_map/ppermute | solution.py:17
  223.3 21.3 %collective-permute-start.30 = (bf16[512,256]{1,0:T(8,128)(2,1)S(1)}, bf16[512,256]{1,0:T(8,128)(2,1)S(1)}, u32[]{:S(2)}, u32[]{:S(2)}) collective-permute-start(bf16[512,256]{1,0:T(8,128)(2,1)S(1)} %attend.5), channel_id=1, source_target_pairs={{0,16},{16,0},{1,17},{17,1},{2,18},{18,2},{3,19},{19,3},{4,20},{20... | collective-permute-start | bytes 786440 | tf_op jit(solution)/shard_map/ppermute | solution.py:17
  (16 other events, 95.1 us)
